TPU v7x, 32 devices: a whole 2x2x4 slice. The times are simulated.
32 devices in a mesh: dp: 8 (over z, y), ep: 4 (over x, core).
Axes of the slice: x: 2, y: 2, z: 4, core: 2. Of those that a mesh axis runs over, the one named last changes fastest.
Arguments:
- w_gate: bfloat16 [1, 16, 2048, 1024], P(None, 'ep')
- w_up: bfloat16 [1, 16, 2048, 1024], P(None, 'ep')
- w_down: bfloat16 [1, 16, 1024, 2048], P(None, 'ep')
- place: int32 [1, 64], replicated
Outputs:
- output 1: bfloat16 [1, 64, 2048, 2048], P(None, ('dp', 'ep'))
- output 2: bfloat16 [1, 64, 1024, 2048], P(None, ('dp', 'ep'))
All inputs are finite; a program needn't handle non-finite values.
Results may differ from a plain program's by a relative error of at most 0.001.
Values are sent between devices in bfloat16 or wider.
A program may use at most 1 GiB of HBM per device.

v0:
```python
import jax
import jax.numpy as jnp
import numpy as np
from jax import lax
from jax.sharding import PartitionSpec as P


def _routes(dp, ep, slots):
    n_dev = dp * ep
    out = []
    for j in range(slots):
        pairs, send_to, local = [], list(range(n_dev)), [False] * n_dev
        for a in range(dp):
            for g in range(ep):
                h = (2 * a - g) % ep if j < ((a + 1) * slots) // dp else (g + j + 1) % ep
                n = a * ep + g
                if h == g:
                    local[n] = True
                    continue
                src = ((a + j) % dp) * ep + h
                pairs.append((src, n))
                send_to[src] = n
        out.append((pairs, send_to, local))
    return out


def solution(mesh):
    dp = mesh.shape["dp"]
    ep = mesh.shape["ep"]
    n_dev = dp * ep

    def body(w_gate, w_up, w_down, place):
        g = lax.axis_index("ep")
        me = lax.axis_index("dp") * ep + g
        n_exp = w_gate.shape[1]
        slots = place.shape[1] // n_dev
        routes = _routes(dp, ep, slots)
        take = jax.vmap(lambda w, i: w[i])
        own = jnp.clip(lax.dynamic_slice_in_dim(place, me * slots, slots, axis=1) - g * n_exp, 0, n_exp - 1)
        own13 = jnp.concatenate([take(w_gate, own), take(w_up, own)], axis=-1)
        own2 = take(w_down, own)
        got13, got2 = [], []
        for j, (pairs, send_to, _) in enumerate(routes):
            dst = jnp.asarray(np.array(send_to, np.int32))[me]
            idx = jnp.clip(place[:, dst * slots + j] - g * n_exp, 0, n_exp - 1)
            b13 = jnp.concatenate([take(w_gate, idx), take(w_up, idx)], axis=-1)
            b2 = take(w_down, idx)
            if pairs:
                b13 = lax.ppermute(b13, ("dp", "ep"), pairs)
                b2 = lax.ppermute(b2, ("dp", "ep"), pairs)
            got13.append(b13)
            got2.append(b2)
        local = jnp.asarray(np.array([r[2] for r in routes], bool).T)[me][None, :, None, None]
        w13 = jnp.where(local, own13, jnp.stack(got13, axis=1))
        w2 = jnp.where(local, own2, jnp.stack(got2, axis=1))
        return w13, w2

    spec_in = P(None, "ep", None, None)
    spec_out = P(None, ("dp", "ep"), None, None)
    return jax.shard_map(body, mesh=mesh,
                         in_specs=(spec_in, spec_in, spec_in, P(None, None)),
                         out_specs=(spec_out, spec_out), check_vma=False)
```

profile of v0, /device:TPU:28, one launch (start us, length us, event | category | flops | bytes accessed | tf_op | source)
XLA Modules:
  0.0 492.0 jit_solution(14330166837239736030)
XLA Ops:
  0.6 1.2 dynamic_slice.20
  2.5 1.2 dynamic_slice.22
  4.4 1.3 constant_dynamic-slice_fusion.1
  7.1 12.3 %dynamic-slice_bitcast_fusion.4 = (bf16[1,2048,1024]{2,1,0:T(8,128)(2,1)}, bf16[1,2048,1024]{2,1,0:T(8,128)(2,1)}, bf16[1,2048,1024]{2,1,0:T(8,128)(2,1)}, bf16[1,2048,1024]{2,1,0:T(8,128)(2,1)}) fusion(bf16[1,4,2048,1024]{3,2,1,0:T(8,128)(2,1)} %param.8, s32[]{:T(128)} %bitcast.12, s32[]{:T(128)} %bitcast.19, bf16[1,4,2048,1024]{3,2,1,0:T(8,128)(2,1)} %param.7), kind=kLoop, calls=%fused_computation.17 | loop fusion | bytes 33554440 | tf_op jit(solution)/shard_map/vmap()/squeeze | solution.py:38
  19.3 8.2 %pad_maximum_fusion = bf16[1,2048,2048]{2,1,0:T(8,128)(2,1)} fusion(bf16[1,2048,1024]{2,1,0:T(8,128)(2,1)} %get-tuple-element.74, bf16[1,2048,1024]{2,1,0:T(8,128)(2,1)} %get-tuple-element.83), kind=kLoop, calls=%fused_computation.10 | loop fusion | flops 16777216 | bytes 16777216 | tf_op jit(solution)/shard_map/concatenate | solution.py:46
  27.5 3.4 collective-permute-start
  30.9 8.3 %pad_maximum_fusion.1 = bf16[1,2048,2048]{2,1,0:T(8,128)(2,1)} fusion(bf16[1,2048,1024]{2,1,0:T(8,128)(2,1)} %get-tuple-element.75, bf16[1,2048,1024]{2,1,0:T(8,128)(2,1)} %get-tuple-element.82), kind=kLoop, calls=%fused_computation.11 | loop fusion | flops 16777216 | bytes 16777216 | tf_op jit(solution)/shard_map/concatenate | solution.py:46
  39.2 3.8 collective-permute-start.1
  43.0 8.4 %dynamic-slice_bitcast_fusion.1 = (bf16[1,1024,2048]{2,1,0:T(8,128)(2,1)}, bf16[1,1024,2048]{2,1,0:T(8,128)(2,1)}) fusion(bf16[1,4,1024,2048]{3,2,1,0:T(8,128)(2,1)} %param.9, s32[]{:T(128)} %bitcast.12, s32[]{:T(128)} %bitcast.19), kind=kLoop, calls=%fused_computation.14 | loop fusion | bytes 16777224 | tf_op jit(solution)/shard_map/vmap()/squeeze | solution.py:38
  51.5 2.2 collective-permute-start.2
  53.6 3.3 collective-permute-start.3
  56.9 4.6 mini-gather-slice.2
  61.5 4.6 mini-gather-slice.5
  66.1 0.0 copy-start.5
  66.1 4.4 mini-gather-slice.8
  70.5 0.0 copy-done.5
  70.5 0.1 fusion.3
  70.6 0.1 copy.11
  70.7 0.1 pad_bitcast_fusion
  70.8 0.2 or_reduce_fusion
  71.0 10.5 %fusion.5 = (bf16[1,4,768,1024]{3,2,1,0:T(8,128)(2,1)}, bf16[1,4,768,1024]{3,2,1,0:T(8,128)(2,1)}) fusion(bf16[1,4,2048,1024]{3,2,1,0:T(8,128)(2,1)} %param.7), kind=kLoop, calls=%fused_computation.31 | loop fusion | bytes 25165824 | tf_op jit(solution)/shard_map/vmap()/gather | solution.py:38
  81.4 3.5 gather_fusion
  85.0 5.3 %gather_fusion.1 = bf16[2,768,1024]{2,1,0:T(8,128)(2,1)} fusion(bf16[1,4,768,1024]{3,2,1,0:T(8,128)(2,1)} %get-tuple-element.77, s32[2]{0:T(128)S(1)} %or_reduce_fusion), kind=kCustom, calls=%fused_computation.1 | custom fusion | bytes 6291472 | tf_op jit(solution)/shard_map/vmap()/gather | solution.py:38
  90.3 10.4 %fusion.6 = (bf16[1,4,768,1024]{3,2,1,0:T(8,128)(2,1)}, bf16[1,4,768,1024]{3,2,1,0:T(8,128)(2,1)}) fusion(bf16[1,4,2048,1024]{3,2,1,0:T(8,128)(2,1)} %param.8), kind=kLoop, calls=%fused_computation.32 | loop fusion | bytes 25165824 | tf_op jit(solution)/shard_map/vmap()/gather | solution.py:38
  100.7 5.2 %gather_fusion.3 = bf16[2,768,1024]{2,1,0:T(8,128)(2,1)} fusion(bf16[1,4,768,1024]{3,2,1,0:T(8,128)(2,1)} %get-tuple-element.78, s32[2]{0:T(128)S(1)} %or_reduce_fusion), kind=kCustom, calls=%fused_computation.3 | custom fusion | bytes 6291472 | tf_op jit(solution)/shard_map/vmap()/gather | solution.py:38
  105.9 5.2 %gather_fusion.4 = bf16[2,768,1024]{2,1,0:T(8,128)(2,1)} fusion(bf16[1,4,768,1024]{3,2,1,0:T(8,128)(2,1)} %get-tuple-element.79, s32[2]{0:T(128)S(1)} %or_reduce_fusion), kind=kCustom, calls=%fused_computation.4 | custom fusion | bytes 6291472 | tf_op jit(solution)/shard_map/vmap()/gather | solution.py:38
  111.1 4.2 gather_fusion.2
  115.3 4.2 gather_fusion.5
  119.6 10.3 %fusion.4 = (bf16[1,4,1024,768]{3,2,1,0:T(8,128)(2,1)}, bf16[1,4,1024,768]{3,2,1,0:T(8,128)(2,1)}) fusion(bf16[1,4,1024,2048]{3,2,1,0:T(8,128)(2,1)} %param.9), kind=kLoop, calls=%fused_computation.30 | loop fusion | bytes 25165824 | tf_op jit(solution)/shard_map/vmap()/gather | solution.py:38
  129.9 5.2 %gather_fusion.6 = bf16[2,1024,768]{2,1,0:T(8,128)(2,1)} fusion(bf16[1,4,1024,768]{3,2,1,0:T(8,128)(2,1)} %get-tuple-element.70, s32[2]{0:T(128)S(1)} %or_reduce_fusion), kind=kCustom, calls=%fused_computation.6 | custom fusion | bytes 6291472 | tf_op jit(solution)/shard_map/vmap()/gather | solution.py:38
  135.1 5.2 %gather_fusion.7 = bf16[2,1024,768]{2,1,0:T(8,128)(2,1)} fusion(bf16[1,4,1024,768]{3,2,1,0:T(8,128)(2,1)} %get-tuple-element.71, s32[2]{0:T(128)S(1)} %or_reduce_fusion), kind=kCustom, calls=%fused_computation.7 | custom fusion | bytes 6291472 | tf_op jit(solution)/shard_map/vmap()/gather | solution.py:38
  140.3 4.2 gather_fusion.8
  144.6 0.7 fusion
  145.2 247.4 %collective-permute-done.2 = bf16[1,1024,2048]{2,1,0:T(8,128)(2,1)} collective-permute-done((bf16[1,1024,2048]{2,1,0:T(8,128)(2,1)}, bf16[1,1024,2048]{2,1,0:T(8,128)(2,1)}, u32[]{:S(2)}, u32[]{:S(2)}) %collective-permute-start.2) | collective-permute-done | bytes 4194336 | tf_op jit(solution)/shard_map/ppermute | solution.py:50
  392.7 43.9 %collective-permute-done.3 = bf16[1,1024,2048]{2,1,0:T(8,128)(2,1)} collective-permute-done((bf16[1,1024,2048]{2,1,0:T(8,128)(2,1)}, bf16[1,1024,2048]{2,1,0:T(8,128)(2,1)}, u32[]{:S(2)}, u32[]{:S(2)}) %collective-permute-start.3) | collective-permute-done | bytes 4194336 | tf_op jit(solution)/shard_map/ppermute | solution.py:50
  436.6 0.0 copy-start
  436.6 0.0 copy-start.1
  436.6 0.0 copy-start.2
  436.6 0.0 copy-start.3
  436.6 0.0 copy-start.4
  436.6 11.3 %maximum_select_fusion.1 = bf16[1,2,1024,2048]{3,2,1,0:T(8,128)(2,1)} fusion(bf16[1,2,1024,512]{3,2,1,0:T(8,128)(2,1)} %bitcast.48, bf16[1,2,1024,768]{3,2,1,0:T(8,128)(2,1)} %bitcast.45, bf16[1,2,1024,768]{3,2,1,0:T(8,128)(2,1)} %bitcast.44, bf16[1,1,1024,2048]{3,2,1,0:T(8,128)(2,1)} %bitcast.29, bf16[1,1,1024,2048]{3,2,1,0:T(8,128)(2,1)} %bitcast.27, ...), kind=kLoop, calls=%fused_computation.12 | loop fusion | flops 46137344 | bytes 25165826 | tf_op jit(solution)/shard_map/jit(_where)/select_n | solution.py:55
  447.9 0.0 collective-permute-done
  447.9 0.0 collective-permute-done.1
  447.9 0.0 copy-done
  447.9 0.0 copy-done.1
  447.9 0.0 copy-done.2
  447.9 1.0 copy-done.3
  449.0 0.6 copy-done.4
  449.5 42.4 %maximum_select_fusion = bf16[1,2,2048,2048]{3,2,1,0:T(8,128)(2,1)} fusion(bf16[1,2,512,1024]{3,2,1,0:T(8,128)(2,1)S(1)} %bitcast.47, bf16[1,2,768,1024]{3,2,1,0:T(8,128)(2,1)S(1)} %bitcast.43, bf16[1,2,768,1024]{3,2,1,0:T(8,128)(2,1)S(1)} %bitcast.42, bf16[1,2,512,1024]{3,2,1,0:T(8,128)(2,1)S(1)} %bitcast.46, bf16[1,2,768,1024]{3,2,1,0:T(8,128)(2,1)S(1)} %bitcast.41, ...), kind=kLoop, calls=%fused_computation.9 | loop fusion | flops 142606336 | bytes 50331648 | tf_op jit(solution)/shard_map/jit(_where)/select_n | solution.py:54
Async XLA Ops:
  27.5 420.4 %collective-permute-start = (bf16[1,2048,2048]{2,1,0:T(8,128)(2,1)}, bf16[1,2048,2048]{2,1,0:T(8,128)(2,1)}, u32[]{:S(2)}, u32[]{:S(2)}) collective-permute-start(bf16[1,2048,2048]{2,1,0:T(8,128)(2,1)} %pad_maximum_fusion), channel_id=1, source_target_pairs={{1,0},{2,1},{3,2},{0,3},{5,4},{6,5},{7,6},{4,7},{9,8},{10,9},{11,1... | collective-permute-start | bytes 25165832 | tf_op jit(solution)/shard_map/ppermute | solution.py:49
  39.2 408.7 %collective-permute-start.1 = (bf16[1,2048,2048]{2,1,0:T(8,128)(2,1)}, bf16[1,2048,2048]{2,1,0:T(8,128)(2,1)}, u32[]{:S(2)}, u32[]{:S(2)}) collective-permute-start(bf16[1,2048,2048]{2,1,0:T(8,128)(2,1)} %pad_maximum_fusion.1), channel_id=1, source_target_pairs={{6,0},{7,1},{4,2},{5,3},{10,4},{11,5},{8,6},{9,7},{14,8},{15,9},{1... | collective-permute-start | bytes 25165832 | tf_op jit(solution)/shard_map/ppermute | solution.py:49
  51.5 341.2 %collective-permute-start.2 = (bf16[1,1024,2048]{2,1,0:T(8,128)(2,1)}, bf16[1,1024,2048]{2,1,0:T(8,128)(2,1)}, u32[]{:S(2)}, u32[]{:S(2)}) collective-permute-start(bf16[1,1024,2048]{2,1,0:T(8,128)(2,1)} %get-tuple-element.68), channel_id=1, source_target_pairs={{1,0},{2,1},{3,2},{0,3},{5,4},{6,5},{7,6},{4,7},{9,8},{10,9},{11,1... | collective-permute-start | bytes 12582920 | tf_op jit(solution)/shard_map/ppermute | solution.py:50
  53.6 383.0 %collective-permute-start.3 = (bf16[1,1024,2048]{2,1,0:T(8,128)(2,1)}, bf16[1,1024,2048]{2,1,0:T(8,128)(2,1)}, u32[]{:S(2)}, u32[]{:S(2)}) collective-permute-start(bf16[1,1024,2048]{2,1,0:T(8,128)(2,1)} %get-tuple-element.69), channel_id=1, source_target_pairs={{6,0},{7,1},{4,2},{5,3},{10,4},{11,5},{8,6},{9,7},{14,8},{15,9},{1... | collective-permute-start | bytes 12582920 | tf_op jit(solution)/shard_map/ppermute | solution.py:50
  66.1 4.4 copy-start.5
  436.6 11.3 %copy-start = (bf16[2,768,1024]{2,1,0:T(8,128)(2,1)S(1)}, bf16[2,768,1024]{2,1,0:T(8,128)(2,1)}, u32[]{:S(2)}) copy-start(bf16[2,768,1024]{2,1,0:T(8,128)(2,1)} %gather_fusion.1) | copy-start | bytes 9437188
  436.6 11.3 %copy-start.1 = (bf16[2,768,1024]{2,1,0:T(8,128)(2,1)S(1)}, bf16[2,768,1024]{2,1,0:T(8,128)(2,1)}, u32[]{:S(2)}) copy-start(bf16[2,768,1024]{2,1,0:T(8,128)(2,1)} %gather_fusion.3) | copy-start | bytes 9437188
  436.6 11.3 %copy-start.2 = (bf16[2,768,1024]{2,1,0:T(8,128)(2,1)S(1)}, bf16[2,768,1024]{2,1,0:T(8,128)(2,1)}, u32[]{:S(2)}) copy-start(bf16[2,768,1024]{2,1,0:T(8,128)(2,1)} %gather_fusion.4) | copy-start | bytes 9437188
  436.6 12.3 %copy-start.3 = (bf16[2,512,1024]{2,1,0:T(8,128)(2,1)S(1)}, bf16[2,512,1024]{2,1,0:T(8,128)(2,1)}, u32[]{:S(2)}) copy-start(bf16[2,512,1024]{2,1,0:T(8,128)(2,1)} %gather_fusion.2) | copy-start | bytes 6291460
  436.6 12.9 %copy-start.4 = (bf16[2,512,1024]{2,1,0:T(8,128)(2,1)S(1)}, bf16[2,512,1024]{2,1,0:T(8,128)(2,1)}, u32[]{:S(2)}) copy-start(bf16[2,512,1024]{2,1,0:T(8,128)(2,1)} %gather_fusion.5) | copy-start | bytes 6291460
where the time goes:
time: 496 us; the launch traced here: 492 us
  waiting for transfers between devices  291 us (59%)
  local copies, waits for them, and re-layouts  114 us (23%)
  other arithmetic  70.4 us (14%)
  starting transfers between devices  12.6 us (3%)
    ppermute x2, waiting for transfers between devices, body(): b2 = lax.ppermute(b2, ('dp', 'ep'), pairs)  291 us
    gather x16, local copies, waits for them, and re-layouts, body(): take = jax.vmap(lambda w, i: w[i])  87.3 us
    select_n x1, other arithmetic, body(): w13 = jnp.where(local, own13, jnp.stack(got13, axis=1))  42.4 us
    squeeze x2, local copies, waits for them, and re-layouts, body(): take = jax.vmap(lambda w, i: w[i])  20.7 us
    concatenate x2, other arithmetic, body(): b13 = jnp.concatenate([take(w_gate, idx), take(w_up, idx)], axis=-1)  16.5 us
    select_n x1, other arithmetic, body(): w2 = jnp.where(local, own2, jnp.stack(got2, axis=1))  11.3 us
  transfers between devices with their start and end apart: 4, of which 2 were waited for; matrix products, arithmetic and copies ran while one was open for 24% of the time, Pallas kernels for 0%

commit v1 on v0

v1 whole, which is shorter than its diff:
```python
import functools

import jax
import jax.numpy as jnp
from jax import lax
from jax.experimental import pallas as pl
from jax.experimental.pallas import tpu as pltpu
from jax.sharding import PartitionSpec as P

UNITS = 32
RING = 4
ORING = 4
DSTAGE = 32
HUB = ((3, 2, 8, 8, 4, 4, 1, 2), (0, 0, 0, 0, 8, 8, 8, 8))
SERVE = (
    ((3, 3, 3, 3, 2, 2, 0, 0), (2, 2, 2, 2, 1, 2, 0, 2), (8, 8, 8, 8, 8, 8, 8, 6), (8, 8, 8, 8, 8, 8, 1, 8),
     (4, 0, 4, 4, 4, 4, 4, 4), (0, 4, 3, 4, 4, 4, 4, 4), (0, 0, 0, 0, 1, 1, 1, 1), (0, 0, 0, 0, 2, 2, 2, 2)),
    ((0, 0, 0, 0, 0, 0, 0, 0), (0, 0, 0, 0, 0, 0, 0, 0), (0, 0, 0, 0, 0, 0, 0, 0), (0, 0, 0, 0, 0, 0, 0, 0),
     (8, 0, 8, 4, 8, 8, 8, 0), (0, 4, 8, 8, 8, 8, 8, 0), (0, 0, 6, 0, 8, 8, 8, 0), (0, 0, 0, 8, 8, 8, 8, 0)),
)
KIND = []
for _a in range(8):
    _row = []
    for _c in range(2):
        for _j in range(2):
            _g = _c + 2
            _h = (2 * _a - _g) % 4 if _j < ((_a + 1) * 2) // 8 else (_g + _j + 1) % 4
            _row.append(_h if _h < 2 else (3 if _h == _g else 2))
    KIND.append(_row)
SLOTS = tuple(tuple((a, s // 2, s % 2) for a in range(8) for s in range(4) if KIND[a][s] == c) for c in range(2))
MAXS = max(len(s) for s in SLOTS)
FIRST = tuple(tuple(sum(HUB[c][:v]) for v in range(8)) for c in range(2))


def _direct(c, u):
    if not any(s[0] == u for s in SLOTS[c]):
        return []
    out = []
    for v in range(8):
        lo, hi = FIRST[c][v] + SERVE[c][v][u], FIRST[c][v] + HUB[c][v]
        if lo == hi:
            continue
        if out and out[-1][1] == lo:
            out[-1][1] = hi
        else:
            out.append([lo, hi])
    return out


DIRECT = tuple(tuple(_direct(c, u) for u in range(8)) for c in range(2))
NDIR = tuple(tuple(sum(hi - lo for lo, hi in r) for r in DIRECT[c]) for c in range(2))


def _pick(table, i):
    r = jnp.int32(table[0])
    for k in range(1, len(table)):
        if table[k] != table[0]:
            r = jnp.where(i == k, jnp.int32(table[k]), r)
    return r


def _remote(place, wg, wu, wd, r13, r2, raw_g, raw_u, raw_d, dw_g, dw_u, dw_d, wk13, wk2, hs_g, hs_u, hs_d,
            ds_g, ds_u, ds_d, os_g, os_u, os_d, raw_rx, raw_tx, h_tx, d_tx, o_tx, ld, rx):
    a = lax.axis_index("dp")
    g = lax.axis_index("ep")
    x = g // 2
    core = g % 2
    w, raw, dw = (wg, wu, wd), (raw_g, raw_u, raw_d), (dw_g, dw_u, dw_d)
    hs, ds, os_, wk = (hs_g, hs_u, hs_d), (ds_g, ds_u, ds_d), (os_g, os_u, os_d), (wk13, wk13, wk2)
    nexp, f = wg.shape[1], wg.shape[3]
    rows = tuple(r.shape[2] for r in raw)

    def expert(s, h):
        return jnp.clip(place[0, s] - h * nexp, 0, nexp - 1)

    def unit(t, k):
        return pl.ds(pl.multiple_of(k * rows[t], rows[t]), rows[t])

    def landing(t, j, k):
        if t == 2:
            return r2.at[j, unit(t, k)]
        return r13.at[j, unit(t, k), pl.ds(t * f, f)]

    def send(t, src, j, k, tx, ua, uep):
        return pltpu.make_async_remote_copy(
            src_ref=src, dst_ref=landing(t, j, k), send_sem=tx, recv_sem=rx.at[j, t],
            device_id={"dp": ua, "ep": uep}, device_id_type=pl.DeviceIdType.MESH)

    for c in range(2):

        @pl.when(core == c)
        def _(c=c):
            width = _pick(HUB[c], a)
            first = _pick(FIRST[c], a)
            slots = SLOTS[c]
            served = [_pick([SERVE[c][v][s[0]] for v in range(8)], a) for s in slots]

            def raw_copy(i, t):
                return pltpu.make_async_remote_copy(
                    src_ref=w[t].at[0, :, unit(t, first + i)], dst_ref=raw[t].at[i],
                    send_sem=raw_tx.at[t, i], recv_sem=raw_rx.at[t, i],
                    device_id={"dp": a, "ep": 2 * (1 - x) + c}, device_id_type=pl.DeviceIdType.MESH)

            def raw_start(i, _):
                for t in range(3):
                    raw_copy(i, t).start()
                return _

            lax.fori_loop(0, width, raw_start, 0)

            dslots = [[(s[1], s[2]) for s in slots if s[0] == u] if NDIR[c][u] else [] for u in range(8)]
            per = max(len(s) for s in dslots)
            ndir = _pick(NDIR[c], a)
            nranges = max(len(r) for r in DIRECT[c])
            starts, steps = [], []
            base = _pick([r[0][0] if r else 0 for r in DIRECT[c]], a)
            for q in range(1, nranges):
                starts.append(_pick([sum(hi - lo for lo, hi in r[:q]) if len(r) > q else 999 for r in DIRECT[c]], a))
                steps.append(_pick([r[q][0] - r[q - 1][1] if len(r) > q else 0 for r in DIRECT[c]], a))

            nown = _pick([UNITS if 2 in KIND[u][:2] else 0 for u in range(8)], a) if c == 1 else jnp.int32(0)
            njobs = ndir + nown

            def dunit(n):
                k = base + n
                for st, sp in zip(starts, steps):
                    k = k + jnp.where(n >= st, sp, 0)
                if c == 1:
                    k = jnp.where(n >= ndir, n - ndir, k)
                return k

            def load(n, t):
                return pltpu.make_async_copy(w[t].at[0, :, unit(t, dunit(n))], dw[t].at[n % 2], ld.at[t, n % 2])

            dtab = []
            for q in range(per):
                dtab.append((_pick([len(s) > q for s in dslots], a),
                             _pick([s[q][0] if len(s) > q else 0 for s in dslots], a),
                             _pick([s[q][1] if len(s) > q else 0 for s in dslots], a)))

            def dsend(n, t, q):
                _, uc, j = dtab[q]
                return send(t, ds[t].at[n * per + q], j, dunit(n), d_tx.at[t, n * per + q], a, 2 * (1 - x) + uc)

            def osend(n, t):
                return send(t, os_[t].at[n % ORING], 0, n, o_tx.at[t, n % ORING], a, 2 * x)

            @pl.when(njobs > 0)
            def _():
                for t in range(3):
                    load(0, t).start()

            def direct(n):
                for t in range(3):
                    load(n, t).wait()
                    wk[t][...] = dw[t][n % 2]

                    @pl.when(n + 1 < njobs)
                    def _():
                        load(n + 1, t).start()

                    @pl.when(n < ndir)
                    def _():
                        for q in range(per):
                            on, uc, j = dtab[q]

                            @pl.when(on == 1)
                            def _():
                                e = expert((a * 4 + 2 * (1 - x) + uc) * 2 + j, 2 * x + c)
                                ds[t][n * per + q] = wk[t][e]

                        for q in range(per):

                            @pl.when(dtab[q][0] == 1)
                            def _():
                                dsend(n, t, q).start()

                    if c == 1:

                        @pl.when(n >= ndir)
                        def _():
                            m = n - ndir

                            @pl.when(m >= ORING)
                            def _():
                                osend(m - ORING, t).wait_send()

                            e = expert((a * 4 + 2 * x) * 2, 2 * x + c)
                            os_[t][m % ORING] = wk[t][e]
                            osend(m, t).start()

            def hub_copy(i, t, q):
                ua, uc, j = slots[q]
                src, tx = hs[t].at[i % RING, q], h_tx.at[t, i % RING, q]
                there = send(t, src, j, first + i, tx, ua, 2 * x + uc)
                here = pltpu.make_async_copy(src, landing(t, j, first + i), tx) if uc == c else None
                return there, here

            def hub_do(i, t, q, start):
                ua, uc, _ = slots[q]
                there, here = hub_copy(i, t, q)
                if here is None:
                    there.start() if start else there.wait_send()
                    return

                @pl.when(a == ua)
                def _():
                    here.start() if start else here.wait()

                @pl.when(a != ua)
                def _():
                    there.start() if start else there.wait_send()

            def hub_free(i, t):
                for q in range(len(slots)):

                    @pl.when(i < served[q])
                    def _():
                        hub_do(i, t, q, False)

            def hub(i):
                for t in range(3):

                    @pl.when(i >= RING)
                    def _():
                        hub_free(i - RING, t)

                    raw_copy(i, t).wait_recv()
                    wk[t][...] = raw[t][i]
                    for q in range(len(slots)):
                        ua, uc, j = slots[q]

                        @pl.when(i < served[q])
                        def _():
                            e = expert((ua * 4 + 2 * x + uc) * 2 + j, 2 * (1 - x) + c)
                            hs[t][i % RING, q] = wk[t][e]

                    for q in range(len(slots)):

                        @pl.when(i < served[q])
                        def _():
                            hub_do(i, t, q, True)

            def step(i, _):
                @pl.when(i < njobs)
                def _():
                    direct(i)

                @pl.when(i < width)
                def _():
                    hub(i)

                return _

            lax.fori_loop(0, jnp.maximum(width, njobs), lambda i, s: (step(i, s), s)[1], 0)

            def hub_drain(i, s):
                for t in range(3):
                    hub_free(i, t)
                return s

            lax.fori_loop(jnp.maximum(width - RING, 0), width, hub_drain, 0)

            def direct_drain(n, s):
                for t in range(3):
                    for q in range(per):

                        @pl.when(dtab[q][0] == 1)
                        def _():
                            dsend(n, t, q).wait_send()
                return s

            lax.fori_loop(0, ndir, direct_drain, 0)
            if c == 1:

                def own_drain(n, s):
                    for t in range(3):
                        osend(n, t).wait_send()
                    return s

                lax.fori_loop(jnp.maximum(nown - ORING, 0), nown, own_drain, 0)

            def raw_drain(i, s):
                for t in range(3):
                    raw_copy(i, t).wait_send()
                return s

            lax.fori_loop(0, width, raw_drain, 0)

            for u in range(8):

                @pl.when(a == u)
                def _(u=u):
                    for j in range(2):
                        kind = KIND[u][2 * c + j]
                        if kind == 3:
                            continue
                        n = UNITS - (SERVE[c][u][u] if kind == c else 0)
                        for t in range(3):
                            if t == 2:
                                part = r2.at[j, pl.ds(0, n * rows[2])]
                            else:
                                part = r13.at[j, pl.ds(0, n * rows[t]), pl.ds(t * f, f)]
                            pltpu.make_async_copy(part, part, rx.at[j, t]).wait()


def _local(nblk, place, wg, wu, wd, r13, r2, o13, o2, buf, lsem, ssem):
    a = lax.axis_index("dp")
    g = lax.axis_index("ep")
    nexp, f = wg.shape[1], wg.shape[3]
    b13 = r13.shape[1] // nblk[0]
    b2 = r2.shape[1] // nblk[1]
    n = 0
    jobs = []
    for j in range(2):
        own = jnp.int32(0)
        for u in range(8):
            for c in range(2):
                if KIND[u][2 * c + j] == 3:
                    own = jnp.where((a == u) & (g % 2 == c), 1, own)
        e = jnp.clip(place[0, (a * 4 + g) * 2 + j] - g * nexp, 0, nexp - 1)
        for b in range(nblk[0] + nblk[1]):
            jobs.append((n, j, b, own, e))
            n += 1
    for n, j, b, own, e in jobs:
        wide = b < nblk[0]
        r = pl.ds(b * b13, b13) if wide else pl.ds((b - nblk[0]) * b2, b2)

        @pl.when(own == 1)
        def _():
            if wide:
                pltpu.make_async_copy(wg.at[0, e, r], buf.at[n, :, pl.ds(0, f)], lsem.at[n]).start()
                pltpu.make_async_copy(wu.at[0, e, r], buf.at[n, :, pl.ds(f, f)], lsem.at[n]).start()
            else:
                pltpu.make_async_copy(wd.at[0, e, r], buf.at[n], lsem.at[n]).start()

        @pl.when(own == 0)
        def _():
            pltpu.make_async_copy((r13 if wide else r2).at[j, r], buf.at[n], lsem.at[n]).start()

    stores = []
    for n, j, b, own, e in jobs:
        wide = b < nblk[0]
        r = pl.ds(b * b13, b13) if wide else pl.ds((b - nblk[0]) * b2, b2)
        pltpu.make_async_copy(buf.at[n], buf.at[n], lsem.at[n]).wait()
        st = pltpu.make_async_copy(buf.at[n], (o13 if wide else o2).at[0, j, r], ssem.at[n])
        st.start()
        stores.append(st)
    for st in stores:
        st.wait()


def solution(mesh):
    anyspec = pl.BlockSpec(memory_space=pl.ANY)
    smem = pl.BlockSpec(memory_space=pltpu.SMEM)

    def body(wg, wu, wd, place):
        _, nexp, d, f = wg.shape
        dt = wg.dtype
        ra, rb = d // UNITS, f // UNITS
        wmax = max(max(h) for h in HUB)
        dma = pltpu.SemaphoreType.DMA

        def three(*lead):
            return [pltpu.VMEM((*lead, ra, f), dt), pltpu.VMEM((*lead, ra, f), dt), pltpu.VMEM((*lead, rb, d), dt)]

        r13, r2 = pl.pallas_call(
            _remote,
            out_shape=(jax.ShapeDtypeStruct((2, d, 2 * f), dt), jax.ShapeDtypeStruct((2, f, d), dt)),
            in_specs=[smem, anyspec, anyspec, anyspec],
            out_specs=(anyspec, anyspec),
            scratch_shapes=[
                *three(wmax, nexp), *three(2, nexp),
                pltpu.VMEM((nexp, ra, f), dt), pltpu.VMEM((nexp, rb, d), dt),
                *three(RING, MAXS), *three(DSTAGE), *three(ORING),
                dma((3, wmax)), dma((3, wmax)), dma((3, RING, MAXS)), dma((3, DSTAGE)), dma((3, ORING)),
                dma((3, 2)), dma((2, 3)),
            ],
            compiler_params=pltpu.CompilerParams(has_side_effects=True, vmem_limit_bytes=62 * 1024 * 1024),
            name="spread",
        )(place, wg, wu, wd)
        nblk = (8, 4)
        nbuf = 2 * sum(nblk)
        return pl.pallas_call(
            functools.partial(_local, nblk),
            out_shape=(jax.ShapeDtypeStruct((1, 2, d, 2 * f), dt), jax.ShapeDtypeStruct((1, 2, f, d), dt)),
            in_specs=[smem, anyspec, anyspec, anyspec, anyspec, anyspec],
            out_specs=(anyspec, anyspec),
            scratch_shapes=[pltpu.VMEM((nbuf, d // nblk[0], 2 * f), dt), dma((nbuf,)), dma((nbuf,))],
            compiler_params=pltpu.CompilerParams(vmem_limit_bytes=48 * 1024 * 1024),
            name="settle",
        )(place, wg, wu, wd, r13, r2)

    spec_in = P(None, "ep", None, None)
    spec_out = P(None, ("dp", "ep"), None, None)
    return jax.shard_map(body, mesh=mesh, in_specs=(spec_in, spec_in, spec_in, P(None, None)),
                         out_specs=(spec_out, spec_out), check_vma=False)
```

time: 496 us -> 269 us (0.54)
  waiting for transfers between devices: 291 us -> 0 us
  Pallas kernels: 0 us -> 265 us
  local copies, waits for them, and re-layouts: 114 us -> 0.01 us
  other arithmetic: 70.4 us -> 0 us
  starting transfers between devices: 12.6 us -> 0 us
    ppermute x4 -> x0, waiting for transfers between devices: 291 us -> none  [the longest x2 291 us: body(): b2 = lax.ppermute(b2, ('dp', 'ep'), pairs)]
    pallas_call x0 -> x2, Pallas kernels: none -> 265 us  [the longest x1 247 us: body(): pl.pallas_call(_remote, out_shape=(jax.ShapeDtypeStruct((2, d, 2 * f), dt...]
    gather x16 -> x0, local copies, waits for them, and re-layouts: 87.3 us -> none  [body(): take = jax.vmap(lambda w, i: w[i])]
    select_n x2 -> x0, other arithmetic: 53.7 us -> none  [the longest x1 42.4 us: body(): w13 = jnp.where(local, own13, jnp.stack(got13, axis=1))]
    squeeze x2 -> x0, local copies, waits for them, and re-layouts: 20.7 us -> none  [body(): take = jax.vmap(lambda w, i: w[i])]
    concatenate x2 -> x0, other arithmetic: 16.5 us -> none  [body(): b13 = jnp.concatenate([take(w_gate, idx), take(w_up, idx)], axis=-1)]
    ppermute x4 -> x0, starting transfers between devices: 12.6 us -> none  [the longest x2 7.2 us: body(): b13 = lax.ppermute(b13, ('dp', 'ep'), pairs)]
  transfers between devices with their start and end apart: 4 -> 0, of which waited for: 2 -> 0; matrix products, arithmetic and copies ran while one was open for 24% -> 0% of each run, Pallas kernels for 0% -> 0%
where the time goes in v1:
time: 269 us; the launch traced here: 266 us
  Pallas kernels  265 us (99%)
    pallas_call x1, Pallas kernels, body(): pl.pallas_call(_remote, out_shape=(jax.ShapeDtypeStruct((2, d, 2 * f), dt...  247 us
    pallas_call x1, Pallas kernels, body(): pl.pallas_call(functools.partial(_local, nblk), out_shape=(jax.ShapeDtype...  18.1 us

profile of v1, /device:TPU:28, one launch (start us, length us, event | category | flops | bytes accessed | tf_op | source)
XLA Modules:
  0.0 265.6 jit_solution(13969230296628755400)
XLA Ops:
  0.6 0.0 copy-start
  0.6 246.9 %spread.1 = (bf16[2,2048,2048]{2,1,0:T(8,128)(2,1)}, bf16[2,1024,2048]{2,1,0:T(8,128)(2,1)}) custom-call(s32[1,64]{1,0:T(1,128)} %place.3, bf16[1,4,2048,1024]{3,2,1,0:T(8,128)(2,1)} %wg.3, bf16[1,4,2048,1024]{3,2,1,0:T(8,128)(2,1)} %wu.3, bf16[1,4,1024,2048]{3,2,1,0:T(8,128)(2,1)} %wd.3), custom_call_target="tpu_custom_call" | custom-call | tf_op jit(solution)/shard_map/spread/pallas_call | solution.py:367
  247.5 0.0 copy-done
  247.5 18.1 %settle.1 = (bf16[1,2,2048,2048]{3,2,1,0:T(8,128)(2,1)}, bf16[1,2,1024,2048]{3,2,1,0:T(8,128)(2,1)}) custom-call(s32[1,64]{1,0:T(1,128)S(1)} %copy-done, bf16[1,4,2048,1024]{3,2,1,0:T(8,128)(2,1)} %wg.3, bf16[1,4,2048,1024]{3,2,1,0:T(8,128)(2,1)} %wu.3, bf16[1,4,1024,2048]{3,2,1,0:T(8,128)(2,1)} %wd.3, bf16[2,2048,2048]{2,1,0:T(8,128)(2,1)} %get-tuple-element.4.r13, ...), custom_call_target="tpu_custom_call" | custom-call | tf_op jit(solution)/shard_map/settle/pallas_call | solution.py:384
Async XLA Ops:
  0.6 246.9 %copy-start = (s32[1,64]{1,0:T(1,128)S(1)}, s32[1,64]{1,0:T(1,128)}, u32[]{:S(2)}) copy-start(s32[1,64]{1,0:T(1,128)} %place.3) | copy-start | bytes 772

commit v2 on v1

--- a/solution.py
+++ b/solution.py
@@ -7,17 +7,16 @@
 from jax.experimental.pallas import tpu as pltpu
 from jax.sharding import PartitionSpec as P
 
-UNITS = 32
-RING = 4
+SUB = 1
+UNITS = 32 * SUB
+RING = 6 * SUB
 ORING = 4
-DSTAGE = 32
-HUB = ((3, 2, 8, 8, 4, 4, 1, 2), (0, 0, 0, 0, 8, 8, 8, 8))
-SERVE = (
-    ((3, 3, 3, 3, 2, 2, 0, 0), (2, 2, 2, 2, 1, 2, 0, 2), (8, 8, 8, 8, 8, 8, 8, 6), (8, 8, 8, 8, 8, 8, 1, 8),
-     (4, 0, 4, 4, 4, 4, 4, 4), (0, 4, 3, 4, 4, 4, 4, 4), (0, 0, 0, 0, 1, 1, 1, 1), (0, 0, 0, 0, 2, 2, 2, 2)),
-    ((0, 0, 0, 0, 0, 0, 0, 0), (0, 0, 0, 0, 0, 0, 0, 0), (0, 0, 0, 0, 0, 0, 0, 0), (0, 0, 0, 0, 0, 0, 0, 0),
-     (8, 0, 8, 4, 8, 8, 8, 0), (0, 4, 8, 8, 8, 8, 8, 0), (0, 0, 6, 0, 8, 8, 8, 0), (0, 0, 0, 8, 8, 8, 8, 0)),
-)
+OWN = 8 * SUB
+DSTAGE = 28 * SUB
+HUB = ((4, 4, 6, 6, 4, 4, 2, 2), (0, 0, 4, 4, 6, 6, 6, 6))
+SERVE = (((4, 4, 4, 4, 0, 0, 0, 0), (4, 4, 4, 4, 0, 4, 0, 0), (6, 6, 6, 6, 6, 4, 6, 4), (6, 6, 6, 6, 6, 6, 2, 6), (3, 0, 4, 3, 4, 4, 4, 4), (0, 3, 3, 4, 4, 4, 4, 4), (0, 0, 2, 0, 2, 2, 2, 2), (0, 0, 0, 2, 2, 2, 2, 2)), ((0, 0, 0, 0, 0, 0, 0, 0), (0, 0, 0, 0, 0, 0, 0, 0), (4, 4, 4, 4, 4, 4, 4, 0), (4, 4, 4, 4, 2, 4, 0, 0), (6, 0, 6, 6, 6, 6, 6, 0), (0, 6, 6, 6, 6, 6, 6, 0), (0, 0, 6, 0, 6, 6, 6, 0), (0, 0, 0, 6, 6, 6, 6, 0)))
+HUB = tuple(tuple(w * SUB for w in h) for h in HUB)
+SERVE = tuple(tuple(tuple(w * SUB for w in r) for r in h) for h in SERVE)
 KIND = []
 for _a in range(8):
     _row = []
@@ -36,8 +35,8 @@
     if not any(s[0] == u for s in SLOTS[c]):
         return []
     out = []
-    for v in range(8):
-        lo, hi = FIRST[c][v] + SERVE[c][v][u], FIRST[c][v] + HUB[c][v]
+    parts = [(FIRST[c][v] + SERVE[c][v][u], FIRST[c][v] + HUB[c][v]) for v in range(8)]
+    for lo, hi in parts + [(sum(HUB[c]), UNITS)]:
         if lo == hi:
             continue
         if out and out[-1][1] == lo:
@@ -60,7 +59,7 @@
 
 
 def _remote(place, wg, wu, wd, r13, r2, raw_g, raw_u, raw_d, dw_g, dw_u, dw_d, wk13, wk2, hs_g, hs_u, hs_d,
-            ds_g, ds_u, ds_d, os_g, os_u, os_d, raw_rx, raw_tx, h_tx, d_tx, o_tx, ld, rx):
+            ds_g, ds_u, ds_d, os_g, os_u, os_d, raw_rx, raw_tx, h_tx, d_tx, o_tx, ld, rx, clear, head):
     a = lax.axis_index("dp")
     g = lax.axis_index("ep")
     x = g // 2
@@ -106,10 +105,19 @@
                     raw_copy(i, t).start()
                 return _
 
+            if c == 1:
+                pl.semaphore_wait(head, 1)
             lax.fori_loop(0, width, raw_start, 0)
+            if c == 0:
+                @pl.when(width > 0)
+                def _():
+                    raw_copy(0, 0).wait_send()
+
+                pl.semaphore_signal(head, 1, device_id={"dp": a, "ep": 2 * x + 1}, device_id_type=pl.DeviceIdType.MESH)
 
             dslots = [[(s[1], s[2]) for s in slots if s[0] == u] if NDIR[c][u] else [] for u in range(8)]
             per = max(len(s) for s in dslots)
+            count = _pick([max(len(s), 1) for s in dslots], a)
             ndir = _pick(NDIR[c], a)
             nranges = max(len(r) for r in DIRECT[c])
             starts, steps = [], []
@@ -119,18 +127,19 @@
                 steps.append(_pick([r[q][0] - r[q - 1][1] if len(r) > q else 0 for r in DIRECT[c]], a))
 
             nown = _pick([UNITS if 2 in KIND[u][:2] else 0 for u in range(8)], a) if c == 1 else jnp.int32(0)
-            njobs = ndir + nown
+            njobs = nown + ndir
 
             def dunit(n):
                 k = base + n
                 for st, sp in zip(starts, steps):
                     k = k + jnp.where(n >= st, sp, 0)
-                if c == 1:
-                    k = jnp.where(n >= ndir, n - ndir, k)
                 return k
 
+            def junit(n):
+                return jnp.where(n < nown, n, dunit(n - nown)) if c == 1 else dunit(n)
+
             def load(n, t):
-                return pltpu.make_async_copy(w[t].at[0, :, unit(t, dunit(n))], dw[t].at[n % 2], ld.at[t, n % 2])
+                return pltpu.make_async_copy(w[t].at[0, :, unit(t, junit(n))], dw[t].at[n % 2], ld.at[t, n % 2])
 
             dtab = []
             for q in range(per):
@@ -140,7 +149,7 @@
 
             def dsend(n, t, q):
                 _, uc, j = dtab[q]
-                return send(t, ds[t].at[n * per + q], j, dunit(n), d_tx.at[t, n * per + q], a, 2 * (1 - x) + uc)
+                return send(t, ds[t].at[n * count + q], j, dunit(n), d_tx.at[t, n * count + q], a, 2 * (1 - x) + uc)
 
             def osend(n, t):
                 return send(t, os_[t].at[n % ORING], 0, n, o_tx.at[t, n % ORING], a, 2 * x)
@@ -159,35 +168,34 @@
                     def _():
                         load(n + 1, t).start()
 
-                    @pl.when(n < ndir)
+                    @pl.when(n >= nown)
                     def _():
+                        m = n - nown
                         for q in range(per):
                             on, uc, j = dtab[q]
 
                             @pl.when(on == 1)
                             def _():
                                 e = expert((a * 4 + 2 * (1 - x) + uc) * 2 + j, 2 * x + c)
-                                ds[t][n * per + q] = wk[t][e]
+                                ds[t][m * count + q] = wk[t][e]
 
                         for q in range(per):
 
                             @pl.when(dtab[q][0] == 1)
                             def _():
-                                dsend(n, t, q).start()
+                                dsend(m, t, q).start()
 
                     if c == 1:
 
-                        @pl.when(n >= ndir)
+                        @pl.when(n < nown)
                         def _():
-                            m = n - ndir
-
-                            @pl.when(m >= ORING)
+                            @pl.when(n >= ORING)
                             def _():
-                                osend(m - ORING, t).wait_send()
+                                osend(n - ORING, t).wait_send()
 
                             e = expert((a * 4 + 2 * x) * 2, 2 * x + c)
-                            os_[t][m % ORING] = wk[t][e]
-                            osend(m, t).start()
+                            os_[t][n % ORING] = wk[t][e]
+                            osend(n, t).start()
 
             def hub_copy(i, t, q):
                 ua, uc, j = slots[q]
@@ -241,18 +249,39 @@
                         def _():
                             hub_do(i, t, q, True)
 
-            def step(i, _):
-                @pl.when(i < njobs)
-                def _():
-                    direct(i)
-
+            def loop(lo, hi, f):
+                lax.fori_loop(lo, hi, lambda i, s: (f(i), s)[1], 0)
+
+            def mixed(i):
                 @pl.when(i < width)
                 def _():
                     hub(i)
 
-                return _
-
-            lax.fori_loop(0, jnp.maximum(width, njobs), lambda i, s: (step(i, s), s)[1], 0)
+                if c == 1:
+
+                    @pl.when(i * OWN < nown)
+                    def _():
+                        loop(0, OWN, lambda r: direct(i * OWN + r))
+
+            loop(0, jnp.maximum(width, _pick([UNITS // OWN if 2 in KIND[u][:2] else 0 for u in range(8)], a)) if c == 1 else width, mixed)
+
+            def raw_drain(i):
+                for t in range(3):
+                    if c == 0 and t == 0:
+
+                        @pl.when(i > 0)
+                        def _():
+                            raw_copy(i, 0).wait_send()
+                    else:
+                        raw_copy(i, t).wait_send()
+
+            most = jnp.maximum(width - 1, 0)
+            loop(0, most, raw_drain)
+            pl.semaphore_signal(clear, 1, device_id={"dp": a, "ep": 2 * x + 1 - c},
+                                device_id_type=pl.DeviceIdType.MESH)
+            pl.semaphore_wait(clear, 1)
+            loop(nown, njobs, direct)
+            loop(most, width, raw_drain)
 
             def hub_drain(i, s):
                 for t in range(3):
@@ -279,13 +308,6 @@
                     return s
 
                 lax.fori_loop(jnp.maximum(nown - ORING, 0), nown, own_drain, 0)
-
-            def raw_drain(i, s):
-                for t in range(3):
-                    raw_copy(i, t).wait_send()
-                return s
-
-            lax.fori_loop(0, width, raw_drain, 0)
 
             for u in range(8):
 
@@ -374,7 +396,7 @@
                 pltpu.VMEM((nexp, ra, f), dt), pltpu.VMEM((nexp, rb, d), dt),
                 *three(RING, MAXS), *three(DSTAGE), *three(ORING),
                 dma((3, wmax)), dma((3, wmax)), dma((3, RING, MAXS)), dma((3, DSTAGE)), dma((3, ORING)),
-                dma((3, 2)), dma((2, 3)),
+                dma((3, 2)), dma((2, 3)), pltpu.SemaphoreType.REGULAR, pltpu.SemaphoreType.REGULAR,
             ],
             compiler_params=pltpu.CompilerParams(has_side_effects=True, vmem_limit_bytes=62 * 1024 * 1024),
             name="spread",

time: 269 us -> 255 us (0.948)
  Pallas kernels: 265 us -> 253 us
    pallas_call x1, Pallas kernels: 247 us -> 235 us  [body(): pl.pallas_call(_remote, out_shape=(jax.ShapeDtypeStruct((2, d, 2 * f), dt...]
where the time goes in v2:
time: 255 us; the launch traced here: 254 us
  Pallas kernels  253 us (99%)
    pallas_call x1, Pallas kernels, body(): pl.pallas_call(_remote, out_shape=(jax.ShapeDtypeStruct((2, d, 2 * f), dt...  235 us
    pallas_call x1, Pallas kernels, body(): pl.pallas_call(functools.partial(_local, nblk), out_shape=(jax.ShapeDtype...  18.1 us

profile of v2, /device:TPU:28, one launch (start us, length us, event | category | flops | bytes accessed | tf_op | source)
XLA Modules:
  0.0 253.5 jit_solution(9702624092837279505)
XLA Ops:
  0.6 0.0 copy-start
  0.6 234.8 %spread.1 = (bf16[2,2048,2048]{2,1,0:T(8,128)(2,1)}, bf16[2,1024,2048]{2,1,0:T(8,128)(2,1)}) custom-call(s32[1,64]{1,0:T(1,128)} %place.3, bf16[1,4,2048,1024]{3,2,1,0:T(8,128)(2,1)} %wg.3, bf16[1,4,2048,1024]{3,2,1,0:T(8,128)(2,1)} %wu.3, bf16[1,4,1024,2048]{3,2,1,0:T(8,128)(2,1)} %wd.3), custom_call_target="tpu_custom_call" | custom-call | tf_op jit(solution)/shard_map/spread/pallas_call | solution.py:389
  235.4 0.0 copy-done
  235.4 18.1 %settle.1 = (bf16[1,2,2048,2048]{3,2,1,0:T(8,128)(2,1)}, bf16[1,2,1024,2048]{3,2,1,0:T(8,128)(2,1)}) custom-call(s32[1,64]{1,0:T(1,128)S(1)} %copy-done, bf16[1,4,2048,1024]{3,2,1,0:T(8,128)(2,1)} %wg.3, bf16[1,4,2048,1024]{3,2,1,0:T(8,128)(2,1)} %wu.3, bf16[1,4,1024,2048]{3,2,1,0:T(8,128)(2,1)} %wd.3, bf16[2,2048,2048]{2,1,0:T(8,128)(2,1)} %get-tuple-element.4.r13, ...), custom_call_target="tpu_custom_call" | custom-call | tf_op jit(solution)/shard_map/settle/pallas_call | solution.py:406
Async XLA Ops:
  0.6 234.8 %copy-start = (s32[1,64]{1,0:T(1,128)S(1)}, s32[1,64]{1,0:T(1,128)}, u32[]{:S(2)}) copy-start(s32[1,64]{1,0:T(1,128)} %place.3) | copy-start | bytes 772

commit v3 on v2

--- a/solution.py
+++ b/solution.py
@@ -13,10 +13,24 @@
 ORING = 4
 OWN = 8 * SUB
 DSTAGE = 28 * SUB
-HUB = ((4, 4, 6, 6, 4, 4, 2, 2), (0, 0, 4, 4, 6, 6, 6, 6))
-SERVE = (((4, 4, 4, 4, 0, 0, 0, 0), (4, 4, 4, 4, 0, 4, 0, 0), (6, 6, 6, 6, 6, 4, 6, 4), (6, 6, 6, 6, 6, 6, 2, 6), (3, 0, 4, 3, 4, 4, 4, 4), (0, 3, 3, 4, 4, 4, 4, 4), (0, 0, 2, 0, 2, 2, 2, 2), (0, 0, 0, 2, 2, 2, 2, 2)), ((0, 0, 0, 0, 0, 0, 0, 0), (0, 0, 0, 0, 0, 0, 0, 0), (4, 4, 4, 4, 4, 4, 4, 0), (4, 4, 4, 4, 2, 4, 0, 0), (6, 0, 6, 6, 6, 6, 6, 0), (0, 6, 6, 6, 6, 6, 6, 0), (0, 0, 6, 0, 6, 6, 6, 0), (0, 0, 0, 6, 6, 6, 6, 0)))
-HUB = tuple(tuple(w * SUB for w in h) for h in HUB)
-SERVE = tuple(tuple(tuple(w * SUB for w in r) for r in h) for h in SERVE)
+
+def _rows(*digits):
+    return tuple(tuple(SUB * int(d) for d in row) for row in digits)
+
+
+HUB = _rows("56444405", "00666662")
+FWD = _rows("00444400", "00000000")
+THERE = (
+    _rows("00000000", "00000000", "00004444", "00004434",
+          "44440000", "44440000", "00000000", "00000000"),
+    _rows(*[8 * "0"] * 8),
+)
+SERVE = (
+    _rows("55532000", "66660600", "44440000", "44440000",
+          "00004444", "00004444", "00000000", "00154555"),
+    _rows("00000000", "00000000", "66666650", "46666600",
+          "20666660", "04666660", "00606660", "00022220"),
+)
 KIND = []
 for _a in range(8):
     _row = []
@@ -28,6 +42,7 @@
     KIND.append(_row)
 SLOTS = tuple(tuple((a, s // 2, s % 2) for a in range(8) for s in range(4) if KIND[a][s] == c) for c in range(2))
 MAXS = max(len(s) for s in SLOTS)
+ACROSS = tuple(2 * (3 - v // 2) + v % 2 for v in range(8))
 FIRST = tuple(tuple(sum(HUB[c][:v]) for v in range(8)) for c in range(2))
 
 
@@ -35,7 +50,7 @@
     if not any(s[0] == u for s in SLOTS[c]):
         return []
     out = []
-    parts = [(FIRST[c][v] + SERVE[c][v][u], FIRST[c][v] + HUB[c][v]) for v in range(8)]
+    parts = [(FIRST[c][v] + THERE[c][v][u] + SERVE[c][v][u], FIRST[c][v] + HUB[c][v]) for v in range(8)]
     for lo, hi in parts + [(sum(HUB[c]), UNITS)]:
         if lo == hi:
             continue
@@ -54,16 +69,16 @@
     r = jnp.int32(table[0])
     for k in range(1, len(table)):
         if table[k] != table[0]:
-            r = jnp.where(i == k, jnp.int32(table[k]), r)
+            r = lax.select(i == k, jnp.int32(table[k]), r)
     return r
 
 
 def _remote(place, wg, wu, wd, r13, r2, raw_g, raw_u, raw_d, dw_g, dw_u, dw_d, wk13, wk2, hs_g, hs_u, hs_d,
-            ds_g, ds_u, ds_d, os_g, os_u, os_d, raw_rx, raw_tx, h_tx, d_tx, o_tx, ld, rx, clear, head):
+            ds_g, ds_u, ds_d, os_g, os_u, os_d, raw_rx, raw_tx, h_tx, d_tx, o_tx, ld, rx, clear, head, f_tx):
     a = lax.axis_index("dp")
     g = lax.axis_index("ep")
-    x = g // 2
-    core = g % 2
+    x = lax.div(g, 2)
+    core = lax.rem(g, 2)
     w, raw, dw = (wg, wu, wd), (raw_g, raw_u, raw_d), (dw_g, dw_u, dw_d)
     hs, ds, os_, wk = (hs_g, hs_u, hs_d), (ds_g, ds_u, ds_d), (os_g, os_u, os_d), (wk13, wk13, wk2)
     nexp, f = wg.shape[1], wg.shape[3]
@@ -92,7 +107,23 @@
             width = _pick(HUB[c], a)
             first = _pick(FIRST[c], a)
             slots = SLOTS[c]
-            served = [_pick([SERVE[c][v][s[0]] for v in range(8)], a) for s in slots]
+            nfwd = _pick(FWD[c], a)
+            across = _pick(ACROSS, a)
+            nmore = _pick([FWD[c][ACROSS[v]] for v in range(8)], a)
+            wacross = _pick([HUB[c][ACROSS[v]] for v in range(8)], a)
+            shift = _pick([FIRST[c][ACROSS[v]] - HUB[c][v] for v in range(8)], a)
+            low = [_pick([THERE[c][v][s[0]] for v in range(8)], a) for s in slots]
+            high = [_pick([THERE[c][v][s[0]] + SERVE[c][v][s[0]] for v in range(8)], a) for s in slots]
+            more = [_pick([HUB[c][v] + THERE[c][ACROSS[v]][s[0]] for v in range(8)], a) for s in slots]
+
+            def hunit(i):
+                return lax.select(i < width, first, shift) + i
+
+            def forward(i, t):
+                return pltpu.make_async_remote_copy(
+                    src_ref=raw[t].at[i], dst_ref=raw[t].at[wacross + i], send_sem=f_tx.at[t, i],
+                    recv_sem=raw_rx.at[t, wacross + i],
+                    device_id={"dp": across, "ep": g}, device_id_type=pl.DeviceIdType.MESH)
 
             def raw_copy(i, t):
                 return pltpu.make_async_remote_copy(
@@ -132,27 +163,29 @@
             def dunit(n):
                 k = base + n
                 for st, sp in zip(starts, steps):
-                    k = k + jnp.where(n >= st, sp, 0)
+                    k = k + lax.select(n >= st, sp, jnp.int32(0))
                 return k
 
             def junit(n):
-                return jnp.where(n < nown, n, dunit(n - nown)) if c == 1 else dunit(n)
+                return lax.select(n < nown, n, dunit(n - nown)) if c == 1 else dunit(n)
 
             def load(n, t):
-                return pltpu.make_async_copy(w[t].at[0, :, unit(t, junit(n))], dw[t].at[n % 2], ld.at[t, n % 2])
+                return pltpu.make_async_copy(w[t].at[0, :, unit(t, junit(n))], dw[t].at[lax.rem(n, 2)], ld.at[t, lax.rem(n, 2)])
 
             dtab = []
             for q in range(per):
                 dtab.append((_pick([len(s) > q for s in dslots], a),
                              _pick([s[q][0] if len(s) > q else 0 for s in dslots], a),
                              _pick([s[q][1] if len(s) > q else 0 for s in dslots], a)))
+                dtab[q] += (expert((a * 4 + 2 * (1 - x) + dtab[q][1]) * 2 + dtab[q][2], 2 * x + c),)
+            eown = expert((a * 4 + 2 * x) * 2, 2 * x + c)
 
             def dsend(n, t, q):
-                _, uc, j = dtab[q]
+                _, uc, j, _ = dtab[q]
                 return send(t, ds[t].at[n * count + q], j, dunit(n), d_tx.at[t, n * count + q], a, 2 * (1 - x) + uc)
 
             def osend(n, t):
-                return send(t, os_[t].at[n % ORING], 0, n, o_tx.at[t, n % ORING], a, 2 * x)
+                return send(t, os_[t].at[lax.rem(n, ORING)], 0, n, o_tx.at[t, lax.rem(n, ORING)], a, 2 * x)
 
             @pl.when(njobs > 0)
             def _():
@@ -162,7 +195,7 @@
             def direct(n):
                 for t in range(3):
                     load(n, t).wait()
-                    wk[t][...] = dw[t][n % 2]
+                    wk[t][...] = dw[t][lax.rem(n, 2)]
 
                     @pl.when(n + 1 < njobs)
                     def _():
@@ -172,11 +205,9 @@
                     def _():
                         m = n - nown
                         for q in range(per):
-                            on, uc, j = dtab[q]
-
-                            @pl.when(on == 1)
+                            @pl.when(dtab[q][0] == 1)
                             def _():
-                                e = expert((a * 4 + 2 * (1 - x) + uc) * 2 + j, 2 * x + c)
+                                e = dtab[q][3]
                                 ds[t][m * count + q] = wk[t][e]
 
                         for q in range(per):
@@ -193,77 +224,68 @@
                             def _():
                                 osend(n - ORING, t).wait_send()
 
-                            e = expert((a * 4 + 2 * x) * 2, 2 * x + c)
-                            os_[t][n % ORING] = wk[t][e]
+                            os_[t][lax.rem(n, ORING)] = wk[t][eown]
                             osend(n, t).start()
 
-            def hub_copy(i, t, q):
+            picks = [expert((ua * 4 + 2 * x + uc) * 2 + j, 2 * (1 - x) + c) for ua, uc, j in slots]
+
+            def serving(i):
+                mine = i < width
+                zero = jnp.int32(0)
+                return [(i >= lax.select(mine, low[q], zero)) & (i < lax.select(mine, high[q], more[q]))
+                        for q in range(len(slots))]
+
+            def hub_do(p, k, t, q, start):
                 ua, uc, j = slots[q]
-                src, tx = hs[t].at[i % RING, q], h_tx.at[t, i % RING, q]
-                there = send(t, src, j, first + i, tx, ua, 2 * x + uc)
-                here = pltpu.make_async_copy(src, landing(t, j, first + i), tx) if uc == c else None
-                return there, here
-
-            def hub_do(i, t, q, start):
-                ua, uc, _ = slots[q]
-                there, here = hub_copy(i, t, q)
-                if here is None:
-                    there.start() if start else there.wait_send()
+                src, tx = hs[t].at[p, q], h_tx.at[t, p, q]
+
+                def far():
+                    cp = send(t, src, j, k, tx, ua, 2 * x + uc)
+                    cp.start() if start else cp.wait_send()
+
+                if uc != c:
+                    far()
                     return
+                pl.when(a != ua)(far)
 
                 @pl.when(a == ua)
                 def _():
-                    here.start() if start else here.wait()
-
-                @pl.when(a != ua)
-                def _():
-                    there.start() if start else there.wait_send()
-
-            def hub_free(i, t):
+                    cp = pltpu.make_async_copy(src, landing(t, j, k), tx)
+                    cp.start() if start else cp.wait()
+
+            def hub_free(i, on, p, t):
+                k = hunit(i)
                 for q in range(len(slots)):
-
-                    @pl.when(i < served[q])
-                    def _():
-                        hub_do(i, t, q, False)
+                    pl.when(on[q])(functools.partial(hub_do, p, k, t, q, False))
 
             def hub(i):
+                p = lax.rem(i, RING)
+                k = hunit(i)
+                on = serving(i)
                 for t in range(3):
 
                     @pl.when(i >= RING)
                     def _():
-                        hub_free(i - RING, t)
-
-                    raw_copy(i, t).wait_recv()
+                        hub_free(i - RING, serving(i - RING), p, t)
+
+                    pltpu.make_async_copy(raw[t].at[i], raw[t].at[i], raw_rx.at[t, i]).wait()
+
+                    @pl.when(i < nfwd)
+                    def _():
+                        forward(i, t).start()
+
                     wk[t][...] = raw[t][i]
                     for q in range(len(slots)):
-                        ua, uc, j = slots[q]
-
-                        @pl.when(i < served[q])
+
+                        @pl.when(on[q])
                         def _():
-                            e = expert((ua * 4 + 2 * x + uc) * 2 + j, 2 * (1 - x) + c)
-                            hs[t][i % RING, q] = wk[t][e]
+                            hs[t][p, q] = wk[t][picks[q]]
 
                     for q in range(len(slots)):
-
-                        @pl.when(i < served[q])
-                        def _():
-                            hub_do(i, t, q, True)
+                        pl.when(on[q])(functools.partial(hub_do, p, k, t, q, True))
 
             def loop(lo, hi, f):
                 lax.fori_loop(lo, hi, lambda i, s: (f(i), s)[1], 0)
-
-            def mixed(i):
-                @pl.when(i < width)
-                def _():
-                    hub(i)
-
-                if c == 1:
-
-                    @pl.when(i * OWN < nown)
-                    def _():
-                        loop(0, OWN, lambda r: direct(i * OWN + r))
-
-            loop(0, jnp.maximum(width, _pick([UNITS // OWN if 2 in KIND[u][:2] else 0 for u in range(8)], a)) if c == 1 else width, mixed)
 
             def raw_drain(i):
                 for t in range(3):
@@ -276,19 +298,73 @@
                         raw_copy(i, t).wait_send()
 
             most = jnp.maximum(width - 1, 0)
-            loop(0, most, raw_drain)
-            pl.semaphore_signal(clear, 1, device_id={"dp": a, "ep": 2 * x + 1 - c},
-                                device_id_type=pl.DeviceIdType.MESH)
-            pl.semaphore_wait(clear, 1)
-            loop(nown, njobs, direct)
+            early = _pick((0, 0, 1, 1, 1, 1, 0, 0), a)
+
+            def drain_most(i):
+                @pl.when(i < most)
+                def _():
+                    raw_drain(i)
+
+            def direct_some(n):
+                @pl.when(n < njobs)
+                def _():
+                    direct(n)
+
+            def mixed(i):
+                @pl.when(i == most)
+                def _():
+                    loop(0, max(HUB[c]) - 1, drain_most)
+                    pl.semaphore_signal(clear, 1, device_id={"dp": a, "ep": 2 * x + 1 - c},
+                                        device_id_type=pl.DeviceIdType.MESH)
+                    if c == 0:
+
+                        @pl.when(early == 1)
+                        def _():
+                            loop(0, max(NDIR[0]), direct_some)
+
+                def pair(r):
+                    @pl.when(i < lax.select(r == 0, width, nmore))
+                    def _():
+                        hub(i + r * width)
+
+                loop(0, 2, pair)
+                if c == 1:
+
+                    @pl.when(i * OWN < nown)
+                    def _():
+                        loop(0, OWN, lambda r: direct(i * OWN + r))
+
+            ntimes = [max(HUB[c][v], FWD[c][ACROSS[v]], UNITS // OWN if c == 1 and 2 in KIND[v][:2] else 1) for v in range(8)]
+            loop(0, _pick(ntimes, a), mixed)
+
+            if c == 0:
+
+                @pl.when(early == 0)
+                def _():
+                    pl.semaphore_wait(clear, 1)
+                    loop(nown, njobs, direct)
+
+                @pl.when(early == 1)
+                def _():
+                    pl.semaphore_wait(clear, 1)
+            else:
+                pl.semaphore_wait(clear, 1)
+                loop(nown, njobs, direct)
             loop(most, width, raw_drain)
 
+            def forward_drain(i):
+                for t in range(3):
+                    forward(i, t).wait_send()
+
+            loop(0, nfwd, forward_drain)
+
             def hub_drain(i, s):
-                for t in range(3):
-                    hub_free(i, t)
+                on = serving(i)
+                for t in range(3):
+                    hub_free(i, on, lax.rem(i, RING), t)
                 return s
 
-            lax.fori_loop(jnp.maximum(width - RING, 0), width, hub_drain, 0)
+            lax.fori_loop(jnp.maximum(width + nmore - RING, 0), width + nmore, hub_drain, 0)
 
             def direct_drain(n, s):
                 for t in range(3):
@@ -317,7 +393,7 @@
                         kind = KIND[u][2 * c + j]
                         if kind == 3:
                             continue
-                        n = UNITS - (SERVE[c][u][u] if kind == c else 0)
+                        n = UNITS - (SERVE[c][u][u] + THERE[c][ACROSS[u]][u] if kind == c else 0)
                         for t in range(3):
                             if t == 2:
                                 part = r2.at[j, pl.ds(0, n * rows[2])]
@@ -380,7 +456,7 @@
         _, nexp, d, f = wg.shape
         dt = wg.dtype
         ra, rb = d // UNITS, f // UNITS
-        wmax = max(max(h) for h in HUB)
+        wmax = max(HUB[c][v] + FWD[c][ACROSS[v]] for c in range(2) for v in range(8))
         dma = pltpu.SemaphoreType.DMA
 
         def three(*lead):
@@ -396,7 +472,7 @@
                 pltpu.VMEM((nexp, ra, f), dt), pltpu.VMEM((nexp, rb, d), dt),
                 *three(RING, MAXS), *three(DSTAGE), *three(ORING),
                 dma((3, wmax)), dma((3, wmax)), dma((3, RING, MAXS)), dma((3, DSTAGE)), dma((3, ORING)),
-                dma((3, 2)), dma((2, 3)), pltpu.SemaphoreType.REGULAR, pltpu.SemaphoreType.REGULAR,
+                dma((3, 2)), dma((2, 3)), pltpu.SemaphoreType.REGULAR, pltpu.SemaphoreType.REGULAR, dma((3, wmax)),
             ],
             compiler_params=pltpu.CompilerParams(has_side_effects=True, vmem_limit_bytes=62 * 1024 * 1024),
             name="spread",

time: 255 us -> 246 us (0.965)
  Pallas kernels: 253 us -> 245 us
    pallas_call x1, Pallas kernels: 235 us -> 226 us  [body(): pl.pallas_call(_remote, out_shape=(jax.ShapeDtypeStruct((2, d, 2 * f), dt...]
where the time goes in v3:
time: 246 us; the launch traced here: 245 us
  Pallas kernels  245 us (100%)
    pallas_call x1, Pallas kernels, body(): pl.pallas_call(_remote, out_shape=(jax.ShapeDtypeStruct((2, d, 2 * f), dt...  226 us
    pallas_call x1, Pallas kernels, body(): pl.pallas_call(functools.partial(_local, nblk), out_shape=(jax.ShapeDtype...  18.1 us

profile of v3, /device:TPU:28, one launch (start us, length us, event | category | flops | bytes accessed | tf_op | source)
XLA Modules:
  0.0 245.2 jit_solution(12745779830618218339)
XLA Ops:
  0.6 0.0 copy-start
  0.6 226.5 %spread.1 = (bf16[2,2048,2048]{2,1,0:T(8,128)(2,1)}, bf16[2,1024,2048]{2,1,0:T(8,128)(2,1)}) custom-call(s32[1,64]{1,0:T(1,128)} %place.3, bf16[1,4,2048,1024]{3,2,1,0:T(8,128)(2,1)} %wg.3, bf16[1,4,2048,1024]{3,2,1,0:T(8,128)(2,1)} %wu.3, bf16[1,4,1024,2048]{3,2,1,0:T(8,128)(2,1)} %wd.3), custom_call_target="tpu_custom_call" | custom-call | tf_op jit(solution)/shard_map/spread/pallas_call | solution.py:465
  227.1 0.0 copy-done
  227.1 18.1 %settle.1 = (bf16[1,2,2048,2048]{3,2,1,0:T(8,128)(2,1)}, bf16[1,2,1024,2048]{3,2,1,0:T(8,128)(2,1)}) custom-call(s32[1,64]{1,0:T(1,128)S(1)} %copy-done, bf16[1,4,2048,1024]{3,2,1,0:T(8,128)(2,1)} %wg.3, bf16[1,4,2048,1024]{3,2,1,0:T(8,128)(2,1)} %wu.3, bf16[1,4,1024,2048]{3,2,1,0:T(8,128)(2,1)} %wd.3, bf16[2,2048,2048]{2,1,0:T(8,128)(2,1)} %get-tuple-element.4.r13, ...), custom_call_target="tpu_custom_call" | custom-call | tf_op jit(solution)/shard_map/settle/pallas_call | solution.py:482
Async XLA Ops:
  0.6 226.5 %copy-start = (s32[1,64]{1,0:T(1,128)S(1)}, s32[1,64]{1,0:T(1,128)}, u32[]{:S(2)}) copy-start(s32[1,64]{1,0:T(1,128)} %place.3) | copy-start | bytes 772

commit v4 on v3

--- a/solution.py
+++ b/solution.py
@@ -9,7 +9,7 @@
 
 SUB = 1
 UNITS = 32 * SUB
-RING = 6 * SUB
+RING = 4 * SUB
 ORING = 4
 OWN = 8 * SUB
 DSTAGE = 28 * SUB
@@ -74,7 +74,7 @@
 
 
 def _remote(place, wg, wu, wd, r13, r2, raw_g, raw_u, raw_d, dw_g, dw_u, dw_d, wk13, wk2, hs_g, hs_u, hs_d,
-            ds_g, ds_u, ds_d, os_g, os_u, os_d, raw_rx, raw_tx, h_tx, d_tx, o_tx, ld, rx, clear, head, f_tx):
+            ds_g, ds_u, ds_d, os_g, os_u, os_d, raw_rx, raw_tx, h_tx, d_tx, o_tx, ld, rx, clear, head, f_tx, ready):
     a = lax.axis_index("dp")
     g = lax.axis_index("ep")
     x = lax.div(g, 2)
@@ -99,6 +99,40 @@
         return pltpu.make_async_remote_copy(
             src_ref=src, dst_ref=landing(t, j, k), send_sem=tx, recv_sem=rx.at[j, t],
             device_id={"dp": ua, "ep": uep}, device_id_type=pl.DeviceIdType.MESH)
+
+    z, y = lax.div(a, 2), lax.rem(a, 2)
+
+    def tell(sem, dp, ep):
+        pl.semaphore_signal(sem, 1, device_id={"dp": dp, "ep": ep}, device_id_type=pl.DeviceIdType.MESH)
+
+    def tell_z(sem):
+        @pl.when(z > 0)
+        def _():
+            tell(sem, a - 2, g)
+
+        @pl.when(z < 3)
+        def _():
+            tell(sem, a + 2, g)
+
+    nz = _pick((1, 2, 2, 1), z)
+
+    barrier = pltpu.get_barrier_semaphore()
+    other = 2 * x + 1 - core
+    tell(barrier, a, 2 - 2 * x)
+    tell(barrier, a, 3 - 2 * x)
+    tell(barrier, a, other)
+    tell(barrier, 2 * z + 1 - y, g)
+    tell_z(barrier)
+    pl.semaphore_wait(barrier, 4 + nz)
+
+    def meet():
+        for r in range(2):
+            tell_z(ready.at[r])
+            pl.semaphore_wait(ready.at[r], nz)
+        tell(ready.at[2], 2 * z + 1 - y, g)
+        pl.semaphore_wait(ready.at[2], 1)
+        tell(ready.at[3], a, other)
+        pl.semaphore_wait(ready.at[3], 1)
 
     for c in range(2):
 
@@ -136,15 +170,19 @@
                     raw_copy(i, t).start()
                 return _
 
-            if c == 1:
+            if c == 0:
+                lax.fori_loop(0, width, raw_start, 0)
+                meet()
+
+                @pl.when(width > 0)
+                def _():
+                    raw_copy(0, 0).wait_send()
+
+                tell(head, a, g + 1)
+            else:
+                meet()
                 pl.semaphore_wait(head, 1)
-            lax.fori_loop(0, width, raw_start, 0)
-            if c == 0:
-                @pl.when(width > 0)
-                def _():
-                    raw_copy(0, 0).wait_send()
-
-                pl.semaphore_signal(head, 1, device_id={"dp": a, "ep": 2 * x + 1}, device_id_type=pl.DeviceIdType.MESH)
+                lax.fori_loop(0, width, raw_start, 0)
 
             dslots = [[(s[1], s[2]) for s in slots if s[0] == u] if NDIR[c][u] else [] for u in range(8)]
             per = max(len(s) for s in dslots)
@@ -473,8 +511,9 @@
                 *three(RING, MAXS), *three(DSTAGE), *three(ORING),
                 dma((3, wmax)), dma((3, wmax)), dma((3, RING, MAXS)), dma((3, DSTAGE)), dma((3, ORING)),
                 dma((3, 2)), dma((2, 3)), pltpu.SemaphoreType.REGULAR, pltpu.SemaphoreType.REGULAR, dma((3, wmax)),
+                pltpu.SemaphoreType.REGULAR((4,)),
             ],
-            compiler_params=pltpu.CompilerParams(has_side_effects=True, vmem_limit_bytes=62 * 1024 * 1024),
+            compiler_params=pltpu.CompilerParams(has_side_effects=True, collective_id=0, vmem_limit_bytes=62 * 1024 * 1024),
             name="spread",
         )(place, wg, wu, wd)
         nblk = (8, 4)

time: 246 us -> 242 us (0.984)
  Pallas kernels: 245 us -> 240 us
    pallas_call x1, Pallas kernels: 226 us -> 221 us  [body(): pl.pallas_call(_remote, out_shape=(jax.ShapeDtypeStruct((2, d, 2 * f), dt...]
where the time goes in v4:
time: 242 us; the launch traced here: 240 us
  Pallas kernels  240 us (99%)
    pallas_call x1, Pallas kernels, body(): pl.pallas_call(_remote, out_shape=(jax.ShapeDtypeStruct((2, d, 2 * f), dt...  221 us
    pallas_call x1, Pallas kernels, body(): pl.pallas_call(functools.partial(_local, nblk), out_shape=(jax.ShapeDtype...  18.1 us

profile of v4, /device:TPU:28, one launch (start us, length us, event | category | flops | bytes accessed | tf_op | source)
XLA Modules:
  0.0 240.2 jit_solution(13228845277868674239)
XLA Ops:
  0.6 0.0 copy-start
  0.6 221.5 %spread.1 = (bf16[2,2048,2048]{2,1,0:T(8,128)(2,1)}, bf16[2,1024,2048]{2,1,0:T(8,128)(2,1)}) custom-call(s32[1,64]{1,0:T(1,128)} %place.3, bf16[1,4,2048,1024]{3,2,1,0:T(8,128)(2,1)} %wg.3, bf16[1,4,2048,1024]{3,2,1,0:T(8,128)(2,1)} %wu.3, bf16[1,4,1024,2048]{3,2,1,0:T(8,128)(2,1)} %wd.3), custom_call_target="tpu_custom_call" | custom-call | tf_op jit(solution)/shard_map/spread/pallas_call | solution.py:503
  222.1 0.0 copy-done
  222.1 18.1 %settle.1 = (bf16[1,2,2048,2048]{3,2,1,0:T(8,128)(2,1)}, bf16[1,2,1024,2048]{3,2,1,0:T(8,128)(2,1)}) custom-call(s32[1,64]{1,0:T(1,128)S(1)} %copy-done, bf16[1,4,2048,1024]{3,2,1,0:T(8,128)(2,1)} %wg.3, bf16[1,4,2048,1024]{3,2,1,0:T(8,128)(2,1)} %wu.3, bf16[1,4,1024,2048]{3,2,1,0:T(8,128)(2,1)} %wd.3, bf16[2,2048,2048]{2,1,0:T(8,128)(2,1)} %get-tuple-element.4.r13, ...), custom_call_target="tpu_custom_call" | custom-call | tf_op jit(solution)/shard_map/settle/pallas_call | solution.py:521
Async XLA Ops:
  0.6 221.5 %copy-start = (s32[1,64]{1,0:T(1,128)S(1)}, s32[1,64]{1,0:T(1,128)}, u32[]{:S(2)}) copy-start(s32[1,64]{1,0:T(1,128)} %place.3) | copy-start | bytes 772

commit v5 on v4

--- a/solution.py
+++ b/solution.py
@@ -472,18 +472,22 @@
 
         @pl.when(own == 0)
         def _():
-            pltpu.make_async_copy((r13 if wide else r2).at[j, r], buf.at[n], lsem.at[n]).start()
-
-    stores = []
+            if wide:
+                pltpu.make_async_copy(r13.at[j, r], buf.at[n], lsem.at[n]).start()
+            else:
+                pltpu.make_async_copy(r2.at[j, r], o2.at[0, j, r], ssem.at[n]).start()
+
     for n, j, b, own, e in jobs:
         wide = b < nblk[0]
         r = pl.ds(b * b13, b13) if wide else pl.ds((b - nblk[0]) * b2, b2)
-        pltpu.make_async_copy(buf.at[n], buf.at[n], lsem.at[n]).wait()
-        st = pltpu.make_async_copy(buf.at[n], (o13 if wide else o2).at[0, j, r], ssem.at[n])
-        st.start()
-        stores.append(st)
-    for st in stores:
-        st.wait()
+
+        def store():
+            pltpu.make_async_copy(buf.at[n], buf.at[n], lsem.at[n]).wait()
+            pltpu.make_async_copy(buf.at[n], (o13 if wide else o2).at[0, j, r], ssem.at[n]).start()
+
+        store() if wide else pl.when(own == 1)(store)
+    for n, j, b, own, e in jobs:
+        pltpu.make_async_copy(buf.at[n], buf.at[n], ssem.at[n]).wait()
 
 
 def solution(mesh):
@@ -502,7 +506,7 @@
 
         r13, r2 = pl.pallas_call(
             _remote,
-            out_shape=(jax.ShapeDtypeStruct((2, d, 2 * f), dt), jax.ShapeDtypeStruct((2, f, d), dt)),
+            out_shape=(jax.ShapeDtypeStruct((2, d, 2 * f), dt), pltpu.VMEM((2, f, d), dt)),
             in_specs=[smem, anyspec, anyspec, anyspec],
             out_specs=(anyspec, anyspec),
             scratch_shapes=[
@@ -513,9 +517,10 @@
                 dma((3, 2)), dma((2, 3)), pltpu.SemaphoreType.REGULAR, pltpu.SemaphoreType.REGULAR, dma((3, wmax)),
                 pltpu.SemaphoreType.REGULAR((4,)),
             ],
-            compiler_params=pltpu.CompilerParams(has_side_effects=True, collective_id=0, vmem_limit_bytes=62 * 1024 * 1024),
+            compiler_params=pltpu.CompilerParams(has_side_effects=True, collective_id=0, vmem_limit_bytes=52 * 1024 * 1024),
             name="spread",
         )(place, wg, wu, wd)
+        r2 = pltpu.with_memory_space_constraint(r2, pltpu.VMEM)
         nblk = (8, 4)
         nbuf = 2 * sum(nblk)
         return pl.pallas_call(

time: 242 us -> 239 us (0.988)
  Pallas kernels: 240 us -> 237 us
    pallas_call x1, Pallas kernels: 18.1 us -> 15.6 us  [body(): pl.pallas_call(functools.partial(_local, nblk), out_shape=(jax.ShapeDtype...]
where the time goes in v5:
time: 239 us; the launch traced here: 238 us
  Pallas kernels  237 us (99%)
    pallas_call x1, Pallas kernels, body(): pl.pallas_call(_remote, out_shape=(jax.ShapeDtypeStruct((2, d, 2 * f), dt...  222 us
    pallas_call x1, Pallas kernels, body(): pl.pallas_call(functools.partial(_local, nblk), out_shape=(jax.ShapeDtype...  15.6 us

profile of v5, /device:TPU:28, one launch (start us, length us, event | category | flops | bytes accessed | tf_op | source)
XLA Modules:
  0.0 238.0 jit_solution(13266519782452932161)
XLA Ops:
  0.6 221.8 %spread.1 = (bf16[2,2048,2048]{2,1,0:T(8,128)(2,1)}, bf16[2,1024,2048]{2,1,0:T(8,128)(2,1)S(1)}) custom-call(s32[1,64]{1,0:T(1,128)} %place.3, bf16[1,4,2048,1024]{3,2,1,0:T(8,128)(2,1)} %wg.3, bf16[1,4,2048,1024]{3,2,1,0:T(8,128)(2,1)} %wu.3, bf16[1,4,1024,2048]{3,2,1,0:T(8,128)(2,1)} %wd.3), custom_call_target="tpu_custom_call" | custom-call | tf_op jit(solution)/shard_map/spread/pallas_call | solution.py:507
  222.4 15.6 %settle.1 = (bf16[1,2,2048,2048]{3,2,1,0:T(8,128)(2,1)}, bf16[1,2,1024,2048]{3,2,1,0:T(8,128)(2,1)}) custom-call(s32[1,64]{1,0:T(1,128)} %place.3, bf16[1,4,2048,1024]{3,2,1,0:T(8,128)(2,1)} %wg.3, bf16[1,4,2048,1024]{3,2,1,0:T(8,128)(2,1)} %wu.3, bf16[1,4,1024,2048]{3,2,1,0:T(8,128)(2,1)} %wd.3, bf16[2,2048,2048]{2,1,0:T(8,128)(2,1)} %get-tuple-element.4.r13, ...), custom_call_target="tpu_custom_call" | custom-call | tf_op jit(solution)/shard_map/settle/pallas_call | solution.py:526

commit v6 on v5

--- a/solution.py
+++ b/solution.py
@@ -12,7 +12,7 @@
 RING = 4 * SUB
 ORING = 4
 OWN = 8 * SUB
-DSTAGE = 28 * SUB
+DSTAGE = 22 * SUB
 
 def _rows(*digits):
     return tuple(tuple(SUB * int(d) for d in row) for row in digits)
@@ -41,7 +41,6 @@
             _row.append(_h if _h < 2 else (3 if _h == _g else 2))
     KIND.append(_row)
 SLOTS = tuple(tuple((a, s // 2, s % 2) for a in range(8) for s in range(4) if KIND[a][s] == c) for c in range(2))
-MAXS = max(len(s) for s in SLOTS)
 ACROSS = tuple(2 * (3 - v // 2) + v % 2 for v in range(8))
 FIRST = tuple(tuple(sum(HUB[c][:v]) for v in range(8)) for c in range(2))
 
@@ -61,6 +60,8 @@
     return out
 
 
+BUSY = tuple(tuple([q for q, s in enumerate(SLOTS[c]) if SERVE[c][v][s[0]] or THERE[c][ACROSS[v]][s[0]]] for v in range(8)) for c in range(2))
+MAXS = max(len(b) for c in range(2) for b in BUSY[c])
 DIRECT = tuple(tuple(_direct(c, u) for u in range(8)) for c in range(2))
 NDIR = tuple(tuple(sum(hi - lo for lo, hi in r) for r in DIRECT[c]) for c in range(2))
 
@@ -267,6 +268,8 @@
 
             picks = [expert((ua * 4 + 2 * x + uc) * 2 + j, 2 * (1 - x) + c) for ua, uc, j in slots]
 
+            spot = [_pick([b.index(q) if q in b else 0 for b in BUSY[c]], a) for q in range(len(slots))]
+
             def serving(i):
                 mine = i < width
                 zero = jnp.int32(0)
@@ -275,7 +278,7 @@
 
             def hub_do(p, k, t, q, start):
                 ua, uc, j = slots[q]
-                src, tx = hs[t].at[p, q], h_tx.at[t, p, q]
+                src, tx = hs[t].at[p, spot[q]], h_tx.at[t, p, spot[q]]
 
                 def far():
                     cp = send(t, src, j, k, tx, ua, 2 * x + uc)
@@ -317,7 +320,7 @@
 
                         @pl.when(on[q])
                         def _():
-                            hs[t][p, q] = wk[t][picks[q]]
+                            hs[t][p, spot[q]] = wk[t][picks[q]]
 
                     for q in range(len(slots)):
                         pl.when(on[q])(functools.partial(hub_do, p, k, t, q, True))
@@ -473,9 +476,9 @@
         @pl.when(own == 0)
         def _():
             if wide:
-                pltpu.make_async_copy(r13.at[j, r], buf.at[n], lsem.at[n]).start()
+                pltpu.make_async_copy(r13.at[j, r], o13.at[0, j, r], ssem.at[n]).start()
             else:
-                pltpu.make_async_copy(r2.at[j, r], o2.at[0, j, r], ssem.at[n]).start()
+                pltpu.make_async_copy(r2.at[j, r], buf.at[n], lsem.at[n]).start()
 
     for n, j, b, own, e in jobs:
         wide = b < nblk[0]
@@ -485,7 +488,7 @@
             pltpu.make_async_copy(buf.at[n], buf.at[n], lsem.at[n]).wait()
             pltpu.make_async_copy(buf.at[n], (o13 if wide else o2).at[0, j, r], ssem.at[n]).start()
 
-        store() if wide else pl.when(own == 1)(store)
+        pl.when(own == 1)(store) if wide else store()
     for n, j, b, own, e in jobs:
         pltpu.make_async_copy(buf.at[n], buf.at[n], ssem.at[n]).wait()
 
@@ -506,7 +509,7 @@
 
         r13, r2 = pl.pallas_call(
             _remote,
-            out_shape=(jax.ShapeDtypeStruct((2, d, 2 * f), dt), pltpu.VMEM((2, f, d), dt)),
+            out_shape=(pltpu.VMEM((2, d, 2 * f), dt), jax.ShapeDtypeStruct((2, f, d), dt)),
             in_specs=[smem, anyspec, anyspec, anyspec],
             out_specs=(anyspec, anyspec),
             scratch_shapes=[
@@ -517,10 +520,10 @@
                 dma((3, 2)), dma((2, 3)), pltpu.SemaphoreType.REGULAR, pltpu.SemaphoreType.REGULAR, dma((3, wmax)),
                 pltpu.SemaphoreType.REGULAR((4,)),
             ],
-            compiler_params=pltpu.CompilerParams(has_side_effects=True, collective_id=0, vmem_limit_bytes=52 * 1024 * 1024),
+            compiler_params=pltpu.CompilerParams(has_side_effects=True, collective_id=0, vmem_limit_bytes=46 * 1024 * 1024),
             name="spread",
         )(place, wg, wu, wd)
-        r2 = pltpu.with_memory_space_constraint(r2, pltpu.VMEM)
+        r13 = pltpu.with_memory_space_constraint(r13, pltpu.VMEM)
         nblk = (8, 4)
         nbuf = 2 * sum(nblk)
         return pl.pallas_call(
@@ -529,7 +532,7 @@
             in_specs=[smem, anyspec, anyspec, anyspec, anyspec, anyspec],
             out_specs=(anyspec, anyspec),
             scratch_shapes=[pltpu.VMEM((nbuf, d // nblk[0], 2 * f), dt), dma((nbuf,)), dma((nbuf,))],
-            compiler_params=pltpu.CompilerParams(vmem_limit_bytes=48 * 1024 * 1024),
+            compiler_params=pltpu.CompilerParams(vmem_limit_bytes=44 * 1024 * 1024),
             name="settle",
         )(place, wg, wu, wd, r13, r2)
 

time: 239 us -> 236 us (0.987)
  Pallas kernels: 237 us -> 233 us
    pallas_call x1, Pallas kernels: 15.6 us -> 11.8 us  [body(): pl.pallas_call(functools.partial(_local, nblk), out_shape=(jax.ShapeDtype...]
where the time goes in v6:
time: 236 us; the launch traced here: 233 us
  Pallas kernels  233 us (99%)
    pallas_call x1, Pallas kernels, body(): pl.pallas_call(_remote, out_shape=(pltpu.VMEM((2, d, 2 * f), dt), jax.Sha...  221 us
    pallas_call x1, Pallas kernels, body(): pl.pallas_call(functools.partial(_local, nblk), out_shape=(jax.ShapeDtype...  11.8 us

profile of v6, /device:TPU:28, one launch (start us, length us, event | category | flops | bytes accessed | tf_op | source)
XLA Modules:
  0.0 233.3 jit_solution(10542475277387094273)
XLA Ops:
  0.6 220.9 %spread.1 = (bf16[2,2048,2048]{2,1,0:T(8,128)(2,1)S(1)}, bf16[2,1024,2048]{2,1,0:T(8,128)(2,1)}) custom-call(s32[1,64]{1,0:T(1,128)} %place.3, bf16[1,4,2048,1024]{3,2,1,0:T(8,128)(2,1)} %wg.3, bf16[1,4,2048,1024]{3,2,1,0:T(8,128)(2,1)} %wu.3, bf16[1,4,1024,2048]{3,2,1,0:T(8,128)(2,1)} %wd.3), custom_call_target="tpu_custom_call" | custom-call | tf_op jit(solution)/shard_map/spread/pallas_call | solution.py:510
  221.5 11.8 %settle.1 = (bf16[1,2,2048,2048]{3,2,1,0:T(8,128)(2,1)}, bf16[1,2,1024,2048]{3,2,1,0:T(8,128)(2,1)}) custom-call(s32[1,64]{1,0:T(1,128)} %place.3, bf16[1,4,2048,1024]{3,2,1,0:T(8,128)(2,1)} %wg.3, bf16[1,4,2048,1024]{3,2,1,0:T(8,128)(2,1)} %wu.3, bf16[1,4,1024,2048]{3,2,1,0:T(8,128)(2,1)} %wd.3, bf16[2,2048,2048]{2,1,0:T(8,128)(2,1)S(1)} %get-tuple-element.4.r13, ...), custom_call_target="tpu_custom_call" | custom-call | tf_op jit(solution)/shard_map/settle/pallas_call | solution.py:529

commit v7 on v6

--- a/solution.py
+++ b/solution.py
@@ -10,7 +10,7 @@
 SUB = 1
 UNITS = 32 * SUB
 RING = 4 * SUB
-ORING = 4
+ORING = 2
 OWN = 8 * SUB
 DSTAGE = 22 * SUB
 
@@ -209,7 +209,7 @@
                 return lax.select(n < nown, n, dunit(n - nown)) if c == 1 else dunit(n)
 
             def load(n, t):
-                return pltpu.make_async_copy(w[t].at[0, :, unit(t, junit(n))], dw[t].at[lax.rem(n, 2)], ld.at[t, lax.rem(n, 2)])
+                return pltpu.make_async_copy(w[t].at[0, :, unit(t, junit(n))], dw[t], ld.at[t])
 
             dtab = []
             for q in range(per):
@@ -234,7 +234,7 @@
             def direct(n):
                 for t in range(3):
                     load(n, t).wait()
-                    wk[t][...] = dw[t][lax.rem(n, 2)]
+                    wk[t][...] = dw[t][...]
 
                     @pl.when(n + 1 < njobs)
                     def _():
@@ -475,20 +475,16 @@
 
         @pl.when(own == 0)
         def _():
-            if wide:
-                pltpu.make_async_copy(r13.at[j, r], o13.at[0, j, r], ssem.at[n]).start()
-            else:
-                pltpu.make_async_copy(r2.at[j, r], buf.at[n], lsem.at[n]).start()
+            pltpu.make_async_copy((r13 if wide else r2).at[j, r], (o13 if wide else o2).at[0, j, r], ssem.at[n]).start()
 
     for n, j, b, own, e in jobs:
         wide = b < nblk[0]
         r = pl.ds(b * b13, b13) if wide else pl.ds((b - nblk[0]) * b2, b2)
 
-        def store():
+        @pl.when(own == 1)
+        def _():
             pltpu.make_async_copy(buf.at[n], buf.at[n], lsem.at[n]).wait()
             pltpu.make_async_copy(buf.at[n], (o13 if wide else o2).at[0, j, r], ssem.at[n]).start()
-
-        pl.when(own == 1)(store) if wide else store()
     for n, j, b, own, e in jobs:
         pltpu.make_async_copy(buf.at[n], buf.at[n], ssem.at[n]).wait()
 
@@ -509,21 +505,22 @@
 
         r13, r2 = pl.pallas_call(
             _remote,
-            out_shape=(pltpu.VMEM((2, d, 2 * f), dt), jax.ShapeDtypeStruct((2, f, d), dt)),
+            out_shape=(pltpu.VMEM((2, d, 2 * f), dt), pltpu.VMEM((2, f, d), dt)),
             in_specs=[smem, anyspec, anyspec, anyspec],
             out_specs=(anyspec, anyspec),
             scratch_shapes=[
-                *three(wmax, nexp), *three(2, nexp),
+                *three(wmax, nexp), *three(nexp),
                 pltpu.VMEM((nexp, ra, f), dt), pltpu.VMEM((nexp, rb, d), dt),
                 *three(RING, MAXS), *three(DSTAGE), *three(ORING),
                 dma((3, wmax)), dma((3, wmax)), dma((3, RING, MAXS)), dma((3, DSTAGE)), dma((3, ORING)),
-                dma((3, 2)), dma((2, 3)), pltpu.SemaphoreType.REGULAR, pltpu.SemaphoreType.REGULAR, dma((3, wmax)),
+                dma((3,)), dma((2, 3)), pltpu.SemaphoreType.REGULAR, pltpu.SemaphoreType.REGULAR, dma((3, wmax)),
                 pltpu.SemaphoreType.REGULAR((4,)),
             ],
-            compiler_params=pltpu.CompilerParams(has_side_effects=True, collective_id=0, vmem_limit_bytes=46 * 1024 * 1024),
+            compiler_params=pltpu.CompilerParams(has_side_effects=True, collective_id=0, vmem_limit_bytes=39 * 1024 * 1024),
             name="spread",
         )(place, wg, wu, wd)
         r13 = pltpu.with_memory_space_constraint(r13, pltpu.VMEM)
+        r2 = pltpu.with_memory_space_constraint(r2, pltpu.VMEM)
         nblk = (8, 4)
         nbuf = 2 * sum(nblk)
         return pl.pallas_call(
@@ -532,7 +529,7 @@
             in_specs=[smem, anyspec, anyspec, anyspec, anyspec, anyspec],
             out_specs=(anyspec, anyspec),
             scratch_shapes=[pltpu.VMEM((nbuf, d // nblk[0], 2 * f), dt), dma((nbuf,)), dma((nbuf,))],
-            compiler_params=pltpu.CompilerParams(vmem_limit_bytes=44 * 1024 * 1024),
+            compiler_params=pltpu.CompilerParams(vmem_limit_bytes=39 * 1024 * 1024),
             name="settle",
         )(place, wg, wu, wd, r13, r2)
 

time: 236 us -> 235 us (level)
    pallas_call x1, Pallas kernels: 11.8 us -> 9.47 us  [body(): pl.pallas_call(functools.partial(_local, nblk), out_shape=(jax.ShapeDtype...]
where the time goes in v7:
time: 235 us; the launch traced here: 231 us
  Pallas kernels  231 us (98%)
    pallas_call x1, Pallas kernels, body(): pl.pallas_call(_remote, out_shape=(pltpu.VMEM((2, d, 2 * f), dt), pltpu.V...  221 us
    pallas_call x1, Pallas kernels, body(): pl.pallas_call(functools.partial(_local, nblk), out_shape=(jax.ShapeDtype...  9.47 us

profile of v7, /device:TPU:28, one launch (start us, length us, event | category | flops | bytes accessed | tf_op | source)
XLA Modules:
  0.0 231.3 jit_solution(1647463092414717075)
XLA Ops:
  0.6 221.1 %spread.1 = (bf16[2,2048,2048]{2,1,0:T(8,128)(2,1)S(1)}, bf16[2,1024,2048]{2,1,0:T(8,128)(2,1)S(1)}) custom-call(s32[1,64]{1,0:T(1,128)} %place.3, bf16[1,4,2048,1024]{3,2,1,0:T(8,128)(2,1)} %wg.3, bf16[1,4,2048,1024]{3,2,1,0:T(8,128)(2,1)} %wu.3, bf16[1,4,1024,2048]{3,2,1,0:T(8,128)(2,1)} %wd.3), custom_call_target="tpu_custom_call" | custom-call | tf_op jit(solution)/shard_map/spread/pallas_call | solution.py:506
  221.8 9.5 %settle.1 = (bf16[1,2,2048,2048]{3,2,1,0:T(8,128)(2,1)}, bf16[1,2,1024,2048]{3,2,1,0:T(8,128)(2,1)}) custom-call(s32[1,64]{1,0:T(1,128)} %place.3, bf16[1,4,2048,1024]{3,2,1,0:T(8,128)(2,1)} %wg.3, bf16[1,4,2048,1024]{3,2,1,0:T(8,128)(2,1)} %wu.3, bf16[1,4,1024,2048]{3,2,1,0:T(8,128)(2,1)} %wd.3, bf16[2,2048,2048]{2,1,0:T(8,128)(2,1)S(1)} %get-tuple-element.4.r13, ...), custom_call_target="tpu_custom_call" | custom-call | tf_op jit(solution)/shard_map/settle/pallas_call | solution.py:526

commit v8 on v7

--- a/solution.py
+++ b/solution.py
@@ -521,7 +521,7 @@
         )(place, wg, wu, wd)
         r13 = pltpu.with_memory_space_constraint(r13, pltpu.VMEM)
         r2 = pltpu.with_memory_space_constraint(r2, pltpu.VMEM)
-        nblk = (8, 4)
+        nblk = (16, 8)
         nbuf = 2 * sum(nblk)
         return pl.pallas_call(
             functools.partial(_local, nblk),

time: 235 us -> 235 us (level)
  no operation moved by 1% of the time
where the time goes in v8:
time: 235 us; the launch traced here: 232 us
  Pallas kernels  231 us (98%)
    pallas_call x1, Pallas kernels, body(): pl.pallas_call(_remote, out_shape=(pltpu.VMEM((2, d, 2 * f), dt), pltpu.V...  221 us
    pallas_call x1, Pallas kernels, body(): pl.pallas_call(functools.partial(_local, nblk), out_shape=(jax.ShapeDtype...  9.9 us

profile of v8, /device:TPU:28, one launch (start us, length us, event | category | flops | bytes accessed | tf_op | source)
XLA Modules:
  0.0 231.7 jit_solution(4348226457131027733)
XLA Ops:
  0.6 221.1 %spread.1 = (bf16[2,2048,2048]{2,1,0:T(8,128)(2,1)S(1)}, bf16[2,1024,2048]{2,1,0:T(8,128)(2,1)S(1)}) custom-call(s32[1,64]{1,0:T(1,128)} %place.3, bf16[1,4,2048,1024]{3,2,1,0:T(8,128)(2,1)} %wg.3, bf16[1,4,2048,1024]{3,2,1,0:T(8,128)(2,1)} %wu.3, bf16[1,4,1024,2048]{3,2,1,0:T(8,128)(2,1)} %wd.3), custom_call_target="tpu_custom_call" | custom-call | tf_op jit(solution)/shard_map/spread/pallas_call | solution.py:506
  221.8 9.9 %settle.1 = (bf16[1,2,2048,2048]{3,2,1,0:T(8,128)(2,1)}, bf16[1,2,1024,2048]{3,2,1,0:T(8,128)(2,1)}) custom-call(s32[1,64]{1,0:T(1,128)} %place.3, bf16[1,4,2048,1024]{3,2,1,0:T(8,128)(2,1)} %wg.3, bf16[1,4,2048,1024]{3,2,1,0:T(8,128)(2,1)} %wu.3, bf16[1,4,1024,2048]{3,2,1,0:T(8,128)(2,1)} %wd.3, bf16[2,2048,2048]{2,1,0:T(8,128)(2,1)S(1)} %get-tuple-element.4.r13, ...), custom_call_target="tpu_custom_call" | custom-call | tf_op jit(solution)/shard_map/settle/pallas_call | solution.py:526
